TPU v7x, 256 devices: a whole 4x4x8 slice. The times are simulated.
256 devices in a mesh: col: 64 (over z, y, core), row: 4 (over x).
Axes of the slice: x: 4, y: 4, z: 8, core: 2. Of those that a mesh axis runs over, the one named last changes fastest.
Arguments:
- produced_encoder_vectors: bfloat16 [8192, 2048], P(('col', 'row')), may hold values from -7 to 7
- real_embeddings: bfloat16 [8192, 2048], P(('col', 'row')), may hold values from -7 to 7
Outputs:
- drift: float32 [8192, 2048], P(('col', 'row'))
All inputs are finite; a program needn't handle non-finite values.
Results may differ from a plain program's by a relative error of at most 0.0035.
Values may be sent and summed in bfloat16 or wider, within the bound.
A program may use at most 64 MiB of HBM per device.

v0:
```python
import functools

import jax
import jax.numpy as jnp
from jax import lax
from jax.sharding import Mesh
from jax.sharding import PartitionSpec as P

COL = ("col_0", "col_1", "col_2")
COL_ROW = ("col_0", "col_1", "col_2", "row")


laplace_scale_factor = 0.3
masked_logit = -1e30
epsilon = 1e-06


def laid_out(tiles, dim):
    lengths = list(tiles.shape[1:])
    lengths[dim] *= tiles.shape[0]
    return jnp.moveaxis(tiles, 0, dim).reshape(lengths)


def from_everyone(value, axis):
    length = lax.axis_size(axis)
    return lax.all_to_all(
        jnp.broadcast_to(value[None], (length, *value.shape)), axis, 0, 0, tiled=True
    )


def gather_directly(value, axis, dim):
    return laid_out(from_everyone(value, axis), dim)


def side_by_side(arrays, axis, dim, along):
    ends, at = ([], 0)
    for a in arrays[:-1]:
        at += a.shape[along]
        ends.append(at)
    both = jnp.concatenate(arrays, axis=along)
    return tuple(jnp.split(lax.all_gather(both, axis, axis=dim, tiled=True), ends, axis=along))


def all_in_one(value, axis):
    leaves = jax.tree.leaves(value)
    sequence = sorted(range(len(leaves)), key=lambda k: -leaves[k].size)
    width = (1, *leaves[sequence[0]].shape)[-1]
    lines = [
        jnp.pad(leaves[k].reshape(-1), (0, -leaves[k].size % width)).reshape(-1, width)
        for k in sequence
    ]
    both, at, found = (lax.all_gather(jnp.concatenate(lines), axis), 0, {})
    for k, line in zip(sequence, lines):
        slab = both[:, at : at + len(line)].reshape(len(both), -1)
        found[k] = slab[:, : leaves[k].size].reshape(-1, *leaves[k].shape)
        at += len(line)
    numbers = iter(range(len(leaves)))
    return jax.tree.map(lambda _: found[next(numbers)], value)


def combined_by_axis(value, axes, combine):
    for axis in axes:
        pieces = all_in_one(value, axis)
        value = jax.tree.map(lambda part: part[0], pieces)
        for k in range(1, lax.axis_size(axis)):
            value = combine(value, jax.tree.map(lambda part: part[k], pieces))
    return value


def gathered_once(value, axis):
    leaves = jax.tree.leaves(value)
    sequence = sorted(range(len(leaves)), key=lambda k: -leaves[k].size)
    width = (1, *leaves[sequence[0]].shape)[-1]
    lines = [
        jnp.pad(leaves[k].reshape(-1), (0, -leaves[k].size % width)).reshape(-1, width)
        for k in sequence
    ]
    both, at, found = (from_everyone(jnp.concatenate(lines), axis), 0, {})
    for k, line in zip(sequence, lines):
        slab = both[:, at : at + len(line)].reshape(len(both), -1)
        found[k] = slab[:, : leaves[k].size].reshape(-1, *leaves[k].shape)
        at += len(line)
    numbers = iter(range(len(leaves)))
    return jax.tree.map(lambda _: found[next(numbers)], value)


def gathered_by_type(value, axis):
    leaves, found = (jax.tree.leaves(value), {})
    for initial, a in enumerate(leaves):
        if initial not in found:
            alike = [k for k, b in enumerate(leaves) if b.dtype == a.dtype]
            got = (
                gathered_once([leaves[k] for k in alike], axis)
                if len(alike) > 1
                else [from_everyone(a, axis)]
            )
            for k, b in zip(alike, got):
                found[k] = b
    numbers = iter(range(len(leaves)))
    return jax.tree.map(lambda _: found[next(numbers)], value)


def joined_by_halves(pieces, combine):
    while len(jax.tree.leaves(pieces)[0]) > 1:
        pieces = jax.vmap(combine)(
            *(jax.tree.map(lambda part: part[side::2], pieces) for side in (0, 1))
        )
    return jax.tree.map(lambda part: part[0], pieces)


def joined_all(value, axis, combine):
    pieces = gathered_by_type(value, axis)
    return joined_by_halves(pieces, combine)


def in_blocks(value, dim, length):
    lengths = value.shape
    tiles = value.reshape(*lengths[:dim], length, lengths[dim] // length, *lengths[dim + 1 :])
    return jnp.moveaxis(tiles, dim, 0)


def sent_and_summed(value, axis, dim):
    tiles = in_blocks(value, dim, lax.axis_size(axis))
    arrived = lax.all_to_all(tiles, axis, split_axis=0, concat_axis=0, tiled=True)
    return arrived.sum(axis=0)


def over_axes(value, axes):
    return functools.reduce(lax.psum, axes, value)


def squares(values):
    return jnp.sum(jnp.square(values.astype(jnp.float32)), axis=1)


def owned_ids(column_portion, row_part, row_count, per_dev):
    return (
        (column_portion * row_count + row_part) * per_dev
        + jnp.arange(per_dev, dtype=jnp.int32)[None, :]
    ).reshape(-1)


def distance_logits(row_feats, row_sq, target_feature_vectors):
    inner_prod = jnp.einsum(
        "rd,kd->rk", row_feats, target_feature_vectors, preferred_element_type=jnp.float32
    )
    pairwise_gap_norms = (
        row_sq[:, None] + squares(target_feature_vectors)[None, :] - 2.0 * inner_prod
    )
    return -jnp.sqrt(jnp.maximum(pairwise_gap_norms, 1.0)) / laplace_scale_factor


def kernel_logits(row_feats, row_ids, col_gen, col_real, col_ids):
    row_sq = squares(row_feats)
    gen_logits = distance_logits(row_feats, row_sq, col_gen)
    gen_logits = jnp.where(row_ids[:, None] == col_ids[None, :], masked_logit, gen_logits)
    return jnp.concatenate([gen_logits, distance_logits(row_feats, row_sq, col_real)], axis=1)


def column_local(similarity_weights):
    target_maximum_logit = jnp.max(similarity_weights, axis=0)
    return (
        target_maximum_logit,
        jnp.sum(jnp.exp(similarity_weights - target_maximum_logit[None, :]), axis=0),
    )


def pair_combine(former, latter):
    top = jnp.maximum(former[0], latter[0])
    return (top, former[1] * jnp.exp(former[0] - top) + latter[1] * jnp.exp(latter[0] - top))


def quad_combine(former, latter):
    top = jnp.maximum(former[0], latter[0])
    lead = jnp.exp(former[0] - top)
    trail = jnp.exp(latter[0] - top)
    lead_half = jnp.exp(0.5 * (former[0] - top))
    trail_half = jnp.exp(0.5 * (latter[0] - top))
    return (
        top,
        former[1] * lead + latter[1] * trail,
        former[2] * lead_half + latter[2] * trail_half,
        former[3] * lead_half + latter[3] * trail_half,
    )


def half_weights(similarity_weights, row_peak, col_shift):
    return jnp.exp(similarity_weights - 0.5 * row_peak[:, None] - 0.5 * col_shift[None, :])


def local_sums(similarity_weights, weights, row_peak, generated_count):
    return (
        jnp.sum(jnp.exp(similarity_weights - row_peak[:, None]), axis=1),
        jnp.sum(weights[:, :generated_count], axis=1),
        jnp.sum(weights[:, generated_count:], axis=1),
    )


def drift_terms(weights, row_sum, gen_mass, real_mass, col_gen, col_real):
    generated_count = col_gen.shape[0]
    gen_part = (weights[:, :generated_count] * (-real_mass / row_sum)[:, None]).astype(jnp.bfloat16)
    real_part = (weights[:, generated_count:] * (gen_mass / row_sum)[:, None]).astype(jnp.bfloat16)
    return jnp.dot(gen_part, col_gen, preferred_element_type=jnp.float32) + jnp.dot(
        real_part, col_real, preferred_element_type=jnp.float32
    )


def on_device(produced_encoder_vectors, real_embeddings):
    per_dev = produced_encoder_vectors.shape[0]
    width = produced_encoder_vectors.shape[1]
    col_count = lax.axis_size(COL)
    row_count = lax.axis_size("row")
    col_index = lax.axis_index(COL)
    row_index = lax.axis_index("row")
    col_range = jnp.arange(col_count, dtype=jnp.int32)[:, None]
    row_range = jnp.arange(row_count, dtype=jnp.int32)[:, None]
    row_feats = gather_directly(produced_encoder_vectors, "row", 0)
    col_gen, col_real = side_by_side((produced_encoder_vectors, real_embeddings), COL, 0, 1)
    row_ids = owned_ids(col_index, row_range, row_count, per_dev)
    col_ids = owned_ids(col_range, row_index, row_count, per_dev)
    generated_count = col_gen.shape[0]
    similarity_weights = kernel_logits(row_feats, row_ids, col_gen, col_real, col_ids)
    col_local = column_local(similarity_weights)
    target_maximum_logit, col_total = combined_by_axis(
        (col_local[0], col_local[1]), COL, pair_combine
    )
    col_shift = target_maximum_logit + jnp.log(col_total)
    own_peak = jnp.max(similarity_weights, axis=1)
    weights = half_weights(similarity_weights, own_peak, col_shift)
    sums_here = local_sums(similarity_weights, weights, own_peak, generated_count)
    row_peak, row_sum, gen_mass, real_mass = joined_all(
        (own_peak, sums_here[0], sums_here[1], sums_here[2]), "row", quad_combine
    )
    weights = weights * jnp.exp(0.5 * (own_peak - row_peak))[:, None]
    drift_part = drift_terms(weights, row_sum, gen_mass, real_mass, col_gen, col_real)
    raw = sent_and_summed(drift_part, "row", 0)
    drift_potential = over_axes(jnp.sum(raw * raw), COL_ROW)
    entry_count = per_dev * col_count * row_count * width
    return raw / jnp.sqrt(drift_potential / entry_count + epsilon)


def solution(mesh):
    torus = Mesh(
        mesh.devices.reshape(8, 4, 2, mesh.shape["row"]), ("col_0", "col_1", "col_2", "row")
    )
    return jax.shard_map(
        on_device,
        mesh=torus,
        in_specs=(P(COL_ROW, None), P(COL_ROW, None)),
        out_specs=P(COL_ROW, None),
        check_vma=False,
    )
```

profile of v0, /device:TPU:1, one launch (start us, length us, event | category | flops | bytes accessed | tf_op | source)
XLA Modules:
  0.0 254.5 jit_solution(10107265196920484630)
XLA Ops:
  6.5 1.7 pad_maximum_fusion.1
  8.2 1.7 broadcast_in_dim.8
  10.0 4.8 %all-to-all-start = ((bf16[4,32,2048]{2,1,0:T(8,128)(2,1)}), bf16[4,32,2048]{2,1,0:T(8,128)(2,1)S(1)}, u32[]{:S(2)}, u32[]{:S(2)}) async-start(bf16[4,32,2048]{2,1,0:T(8,128)(2,1)} %broadcast_in_dim.8), calls=%async_computation | async-start | bytes 1048576 | tf_op jit(solution)/shard_map/all_to_all | solution.py:26
  14.9 0.1 add.247
  15.1 7.2 %all-to-all-done = bf16[4,32,2048]{2,1,0:T(8,128)(2,1)S(1)} async-done(((bf16[4,32,2048]{2,1,0:T(8,128)(2,1)}), bf16[4,32,2048]{2,1,0:T(8,128)(2,1)S(1)}, u32[]{:S(2)}, u32[]{:S(2)}) %all-to-all-start) | async-done | bytes 524320 | tf_op jit(solution)/shard_map/all_to_all | solution.py:26
  22.3 0.2 multiply_reduce_fusion.2
  22.5 0.1 add.254
  22.6 91.0 %all-gather.8.cloned.1.call-done = bf16[2048,4096]{1,0:T(8,128)(2,1)} async-done(((bf16[32,4096]{1,0:T(8,128)(2,1)}), bf16[2048,4096]{1,0:T(8,128)(2,1)}) %all-gather.8.cloned.1.call-update) | async-done | bytes 16777232 | tf_op jit(solution)/shard_map/all_gather | solution.py:41
  113.6 7.9 %multiply_reduce_fusion.1 = (f32[2048]{0:T(1024)S(1)}, f32[2048]{0:T(1024)S(1)}) fusion(bf16[2048,4096]{1,0:T(8,128)(2,1)} %all-gather.8.cloned.1.call-done), kind=kLoop, calls=%fused_computation.1 | loop fusion | flops 25161728 | bytes 16793600 | tf_op jit(solution)/shard_map/reduce_sum | solution.py:133
  121.5 2.7 %copy-done = bf16[2048,4096]{1,0:T(8,128)(2,1)S(1)} copy-done((bf16[2048,4096]{1,0:T(8,128)(2,1)S(1)}, bf16[2048,4096]{1,0:T(8,128)(2,1)}, u32[]{:S(2)}) %copy-start) | copy-done | bytes 16777240
  124.3 2.5 fusion.114
  126.8 2.7 %fusion.113 = (f32[128]{0:T(128)S(1)}, f32[128,2048]{0,1:T(8,128)S(1)}) fusion(bf16[128,2048]{1,0:T(8,128)(2,1)S(1)} %bitcast.296, bf16[2048,4096]{1,0:T(8,128)(2,1)S(1)} %copy-done, f32[2048]{0:T(1024)S(1)} %get-tuple-element.5, f32[128]{0:T(128)S(1)} %add.254, s32[2048]{0:T(1024)S(1)} %add.253, s32[128]{0:T(128)S(1)} %add.247), kind=kOutput, calls=%fused_computation.141 | convolution fusion | flops 1076100992 | bytes 9979392 | tf_op jit(solution)/shard_map/rd,kd->rk/dot_general | solution.py:144
  129.5 0.6 exponential_reduce_fusion
  130.1 2.6 %exponential_reduce_fusion.1 = f32[4096]{0:T(1024)S(1)} fusion(f32[4096]{0:T(1024)S(1)} %get-tuple-element.8, f32[128,2048]{0,1:T(8,128)S(1)} %get-tuple-element.35, f32[128,2048]{0,1:T(8,128)S(1)} %get-tuple-element.33), kind=kLoop, calls=%fused_computation.29 | loop fusion | flops 1568768 | bytes 2129920 | tf_op jit(solution)/shard_map/reduce_sum | solution.py:164
  132.7 18.8 %all-gather.3 = f32[8,2,4096]{2,1,0:T(2,128)S(1)} all-gather(f32[1,2,4096]{2,1,0:T(2,128)S(1)} %maximum_bitcast_fusion), channel_id=2, replica_groups=mesh['col_0'=8,'col_1'=4,'col_2'=2,'row'=4] {'col_0'}, dimensions={0}, use_global_device_ids=true | all-gather | bytes 294912 | tf_op jit(solution)/shard_map/all_gather | solution.py:52
  151.5 0.4 fusion.73
  151.9 9.1 %all-gather.4 = f32[4,2,4096]{2,1,0:T(2,128)S(1)} all-gather(f32[1,2,4096]{2,1,0:T(2,128)S(1)} %maximum_bitcast_fusion.1), channel_id=3, replica_groups=mesh['col_0'=8,'col_1'=4,'col_2'=2,'row'=4] {'col_1'}, dimensions={0}, use_global_device_ids=true | all-gather | bytes 163840 | tf_op jit(solution)/shard_map/all_gather | solution.py:52
  161.0 0.2 fusion.64
  161.2 10.7 %all-gather.5 = f32[2,2,4096]{2,1,0:T(2,128)S(1)} all-gather(f32[1,2,4096]{2,1,0:T(2,128)S(1)} %maximum_bitcast_fusion.2), channel_id=4, replica_groups=mesh['col_0'=8,'col_1'=4,'col_2'=2,'row'=4] {'col_2'}, dimensions={0}, use_global_device_ids=true | all-gather | bytes 98304 | tf_op jit(solution)/shard_map/all_gather | solution.py:52
  172.0 1.4 subtract_exponential_fusion
  173.4 0.3 slice_reduce_fusion.1
  173.7 7.9 %all_to_all.15 = f32[4,4,128]{2,1,0:T(4,128)S(1)} all-to-all(f32[4,4,128]{2,1,0:T(4,128)S(1)} %broadcast_in_dim.9), channel_id=1, replica_groups=mesh['col_0'=8,'col_1'=4,'col_2'=2,'row'=4] {'row'}, dimensions={0} | all-to-all | bytes 16384 | tf_op jit(solution)/shard_map/all_to_all | solution.py:26
  181.9 0.1 broadcast_multiply_fusion
  182.1 4.7 %fusion = f32[128,2048]{1,0:T(8,128)S(1)} fusion(bf16[2048,4096]{1,0:T(8,128)(2,1)} %all-gather.8.cloned.1.call-done, f32[128,4096]{0,1:T(8,128)S(1)} %broadcast_multiply_fusion, f32[128]{0:T(128)S(1)} %fusion.108), kind=kOutput, calls=%fused_computation.2 | convolution fusion | flops 1074266112 | bytes 10486272 | tf_op jit(solution)/shard_map/dot_general | solution.py:203
  186.7 4.7 %fusion.14 = f32[128,2048]{1,0:T(8,128)S(1)} fusion(f32[128,2048]{1,0:T(8,128)S(1)} %fusion, bf16[2048,4096]{1,0:T(8,128)(2,1)} %all-gather.8.cloned.1.call-done, f32[128,4096]{0,1:T(8,128)S(1)} %broadcast_multiply_fusion, f32[128]{0:T(128)S(1)} %get-tuple-element.11), kind=kOutput, calls=%fused_computation.12 | convolution fusion | flops 1074528256 | bytes 11534848 | tf_op jit(solution)/shard_map/dot_general | solution.py:203
  191.4 15.8 %all_to_all.16 = f32[4,32,2048]{2,1,0:T(8,128)S(1)} all-to-all(f32[4,32,2048]{2,1,0:T(8,128)S(1)} %bitcast.294), channel_id=1, replica_groups=mesh['col_0'=8,'col_1'=4,'col_2'=2,'row'=4] {'row'}, dimensions={0} | all-to-all | bytes 2097152 | tf_op jit(solution)/shard_map/all_to_all | solution.py:124
  207.3 0.7 multiply_reduce_fusion.3
  208.0 12.4 %psum.28 = f32[]{:T(128)} all-reduce(f32[]{:T(128)} %multiply_reduce_fusion.3), channel_id=1, replica_groups=mesh['col_0'=8,'col_1'=4,'col_2'=2,'row'=4] {'col_0'}, use_global_device_ids=true, to_apply=%region_12.13 | all-reduce | flops 1 | bytes 8 | tf_op jit(solution)/shard_map/psum | solution.py:129
  220.4 7.1 %psum.29 = f32[]{:T(128)} all-reduce(f32[]{:T(128)} %psum.28), channel_id=1, replica_groups=mesh['col_0'=8,'col_1'=4,'col_2'=2,'row'=4] {'col_1'}, use_global_device_ids=true, to_apply=%region_13.14 | all-reduce | flops 1 | bytes 8 | tf_op jit(solution)/shard_map/psum | solution.py:129
  227.6 11.2 %psum.30 = f32[]{:T(128)} all-reduce(f32[]{:T(128)} %psum.29), channel_id=1, replica_groups=mesh['col_0'=8,'col_1'=4,'col_2'=2,'row'=4] {'col_2'}, use_global_device_ids=true, to_apply=%region_14.15 | all-reduce | flops 1 | bytes 8 | tf_op jit(solution)/shard_map/psum | solution.py:129
  238.7 7.5 %psum.31 = f32[]{:T(128)} all-reduce(f32[]{:T(128)} %psum.30), channel_id=1, replica_groups=mesh['col_0'=8,'col_1'=4,'col_2'=2,'row'=4] {'row'}, use_global_device_ids=true, to_apply=%region_15.16 | all-reduce | flops 1 | bytes 8 | tf_op jit(solution)/shard_map/psum | solution.py:129
  246.9 0.7 broadcast_divide_fusion
  (31 shorter events, 0.8 us)
Async XLA Ops:
  6.5 107.1 %all-gather.8.cloned.1.call-start = ((), (), s32[]{:S(2)}) async-start(), calls=%async_computation.3 | async-start | bytes 17039360 | tf_op jit(solution)/shard_map/all_gather | solution.py:41
  10.0 12.3 %all-to-all-start = ((bf16[4,32,2048]{2,1,0:T(8,128)(2,1)}), bf16[4,32,2048]{2,1,0:T(8,128)(2,1)S(1)}, u32[]{:S(2)}, u32[]{:S(2)}) async-start(bf16[4,32,2048]{2,1,0:T(8,128)(2,1)} %broadcast_in_dim.8), calls=%async_computation | async-start | bytes 1048576 | tf_op jit(solution)/shard_map/all_to_all | solution.py:26
  113.6 10.7 %copy-start = (bf16[2048,4096]{1,0:T(8,128)(2,1)S(1)}, bf16[2048,4096]{1,0:T(8,128)(2,1)}, u32[]{:S(2)}) copy-start(bf16[2048,4096]{1,0:T(8,128)(2,1)} %all-gather.8.cloned.1.call-done) | copy-start | bytes 50331652
Sparse Core Ops, SparseCore 0:
  10.1 103.4 all-gather.7
where the time goes:
time: 255 us; the launch traced here: 254 us
  blocking collectives  101 us (40%)
  waiting for transfers between devices  98.2 us (39%)
  other arithmetic  17.1 us (7%)
  matrix products  14.6 us (6%)
  between operations  14.2 us (6%)
  local copies, waits for them, and re-layouts  4.99 us (2%)
  starting transfers between devices  4.83 us (2%)
    all_gather x1, waiting for transfers between devices, side_by_side(): lax.all_gather(both, axis, axis=dim, tiled=True)  91 us
    all_gather x3, blocking collectives, all_in_one(): both, at, found = (lax.all_gather(jnp.concatenate(lines), axis), 0, {})  38.6 us
    psum x4, blocking collectives, over_axes(): return functools.reduce(lax.psum, axes, value)  38.2 us
    all_to_all x1, blocking collectives, sent_and_summed(): lax.all_to_all(tiles, axis, split_axis=0, concat_axis=0, tiled=True)  15.8 us
    reduce_sum x2, other arithmetic, squares(): return jnp.sum(jnp.square(values.astype(jnp.float32)), axis=1)  8.11 us
    all_to_all x1, blocking collectives, from_everyone(): lax.all_to_all(jnp.broadcast_to(value[None], (length, *value.shape)), axi...  7.94 us
    all_to_all x1, waiting for transfers between devices, from_everyone(): lax.all_to_all(jnp.broadcast_to(value[None], (length, *value.shape)), axi...  7.15 us
    dot_general x2, matrix products, distance_logits(): jnp.einsum('rd,kd->rk', row_feats, target_feature_vectors, preferred_elem...  5.2 us
  transfers between devices with their start and end apart: 2, of which 2 were waited for; matrix products, arithmetic and copies ran while one was open for 1% of the time, Pallas kernels for 0%

commit v1 on v0

v1 whole, which is shorter than its diff:
```python
import functools

import jax
import jax.numpy as jnp
from jax import lax
from jax.experimental import pallas as pl
from jax.experimental.pallas import tpu as pltpu
from jax.sharding import Mesh
from jax.sharding import PartitionSpec as P

AXES = ("z", "y", "c", "x")
NZ, NY, NC, NX = 8, 4, 2, 4
PER = 32
WIDTH = 2048
ROWS = NX * NY * PER
CHUNK = 2 * NC * PER
COLS = NZ * CHUNK
INV_SCALE = 1.0 / 0.3
MASKED = -1e30
EPS = 1e-6
F32 = jnp.float32
BF16 = jnp.bfloat16


def eye():
    return lax.broadcasted_iota(jnp.int32, (128, 128), 0) == lax.broadcasted_iota(
        jnp.int32, (128, 128), 1
    )


def to_lanes(v):
    return jnp.sum(jnp.where(eye(), jnp.broadcast_to(v, (128, 128)), 0.0), axis=0, keepdims=True)


def to_rows(v):
    return jnp.sum(jnp.where(eye(), jnp.broadcast_to(v, (128, 128)), 0.0), axis=1, keepdims=True)


def kernel(
    gen_ref, real_ref, out_ref,
    rows, cols, logits, signed, rsq, rvec, gvec, mvec, csv,
    cstat, rstat, mstat, n1, n2,
    psend, acc, far1, near1, qsend, far2, near2,
    in_sem, zs, zr, ss, sr, ps, pr, xs, xr, fs, fr,
):
    z, y, c, x = (lax.axis_index(a) for a in AXES)
    p = x * (1 - c) + y * c
    q = y * (1 - c) + x * c

    def at_z(zz):
        return {"z": zz, "y": y, "c": c, "x": x}

    def at_pq(pp, qq):
        return {"z": z, "y": qq * (1 - c) + pp * c, "c": c, "x": pp * (1 - c) + qq * c}

    def zmod(d):
        return lax.rem(z + (d + NZ), NZ)

    def pmod(d):
        return lax.rem(p + (d + 4), 4)

    def qmod(d):
        return lax.rem(q + (d + 4), 4)

    sibling = {"z": z, "y": y, "c": 1 - c, "x": x}
    pending = []

    def send(src, dst, ssem, rsem, dev):
        copy = pltpu.make_async_remote_copy(
            src_ref=src, dst_ref=dst, send_sem=ssem, recv_sem=rsem,
            device_id=dev, device_id_type=pl.DeviceIdType.MESH,
        )
        copy.start()
        pending.append(copy)

    def arrived(ref, sem):
        pltpu.make_async_copy(ref, ref, sem).wait()

    own = q * 4 + p
    loads = (
        pltpu.make_async_copy(gen_ref, rows.at[own], in_sem.at[0]),
        pltpu.make_async_copy(gen_ref, cols.at[z, c, 0], in_sem.at[1]),
        pltpu.make_async_copy(real_ref, cols.at[z, c, 1], in_sem.at[2]),
    )
    for copy in loads:
        copy.start()
    barrier = pltpu.get_barrier_semaphore()
    near = (
        sibling, at_z(zmod(1)), at_z(zmod(-1)),
        at_pq(pmod(1), q), at_pq(pmod(-1), q), at_pq(p, qmod(1)), at_pq(p, qmod(-1)),
    )
    for dev in near:
        pl.semaphore_signal(barrier, inc=1, device_id=dev, device_id_type=pl.DeviceIdType.MESH)
    pl.semaphore_wait(barrier, len(near))
    for copy in loads:
        copy.wait()

    def z_send(d, h, kind):
        s = 1 - 2 * d
        src = cols.at[zmod(-s * (h - 1)), c, kind]
        k = (d * 4 + h - 1) * 2 + kind
        send(src, src, zs.at[k], zr.at[k], at_z(zmod(s)))

    def sib_send(d, h, kind):
        s = 1 - 2 * d
        src = cols.at[zmod(-s * h), c, kind]
        k = (d * 5 + h) * 2 + kind
        send(src, src, ss.at[k], sr.at[k], sibling)

    def z_arrive(h, turn):
        for d in (0, 1):
            s = 1 - 2 * d
            kind = d if turn == 0 else 1 - d
            if h == 4 and turn == 1:
                continue
            arrived(cols.at[zmod(-s * h), c, kind], zr.at[(d * 4 + h - 1) * 2 + kind])
            if h < 3 or (h == 3 and turn == 0):
                z_send(d, h + 1, kind)
            sib_send(d, h, kind)

    def sib_arrive(h):
        for d in (0, 1):
            s = 1 - 2 * d
            if h == 0 and d == 1:
                continue
            for kind in (0, 1):
                if h == 4 and kind != d:
                    continue
                arrived(cols.at[zmod(-s * h), 1 - c, kind], sr.at[(d * 5 + h) * 2 + kind])

    for turn in (0, 1):
        for d in (0, 1):
            z_send(d, 1, d if turn == 0 else 1 - d)
    send(rows.at[own], rows.at[own], ps.at[0], pr.at[0], at_pq(pmod(1), q))
    send(rows.at[own], rows.at[own], ps.at[1], pr.at[1], at_pq(pmod(-1), q))
    sib_send(0, 0, 0)
    sib_send(0, 0, 1)

    left, right = q * 4 + pmod(-1), q * 4 + pmod(1)
    far = q * 4 + pmod(2)
    arrived(rows.at[left], pr.at[0])
    top = rows.at[left, pl.ds(0, 16)]
    send(top, top, ps.at[2], pr.at[2], at_pq(pmod(1), q))
    arrived(rows.at[right], pr.at[1])
    low = rows.at[right, pl.ds(16, 16)]
    send(low, low, ps.at[3], pr.at[3], at_pq(pmod(-1), q))
    z_arrive(1, 0)
    arrived(rows.at[far, pl.ds(0, 16)], pr.at[2])
    arrived(rows.at[far, pl.ds(16, 16)], pr.at[3])
    mine = rows.at[pl.ds(q * 4, 4)]
    send(mine, mine, ps.at[4], pr.at[4], at_pq(p, qmod(1)))
    send(mine, mine, ps.at[5], pr.at[5], at_pq(p, qmod(-1)))
    z_arrive(1, 1)
    z_arrive(2, 0)

    def squares_of(value):
        value = value.astype(F32)
        return jnp.sum(value * value, axis=1, keepdims=True)

    def row_squares(qq):
        def one(k, carry):
            g = qq * 4 + k
            rsq[pl.ds(g * PER, PER), :] = squares_of(rows[g])
            return carry
        lax.fori_loop(0, 4, one, 0)

    def col_squares(zz):
        total = to_lanes(squares_of(cols[zz].reshape(CHUNK, WIDTH)))
        csv[pl.ds(zz, 1), :] = total

    row_squares(q)
    z_arrive(2, 1)
    before, after, across = qmod(-1), qmod(1), qmod(2)
    arrived(rows.at[pl.ds(before * 4, 4)], pr.at[4])
    top = rows.at[pl.ds(before * 4, 2)]
    send(top, top, ps.at[6], pr.at[6], at_pq(p, after))
    arrived(rows.at[pl.ds(after * 4, 4)], pr.at[5])
    low = rows.at[pl.ds(after * 4 + 2, 2)]
    send(low, low, ps.at[7], pr.at[7], at_pq(p, before))
    row_squares(before)
    row_squares(after)
    sib_arrive(0)
    sib_arrive(1)
    sib_arrive(2)
    for d in (0, 1, -1):
        col_squares(zmod(d))
    z_arrive(3, 0)
    col_squares(zmod(2))
    col_squares(zmod(-2))
    arrived(rows.at[pl.ds(across * 4, 2)], pr.at[6])
    arrived(rows.at[pl.ds(across * 4 + 2, 2)], pr.at[7])
    row_squares(across)

    def tile(za, zb):
        rhs = jnp.concatenate(
            [cols[za].reshape(CHUNK, WIDTH), cols[zb].reshape(CHUNK, WIDTH)], axis=0
        )
        inner = lax.dot_general(
            rows[...].reshape(ROWS, WIDTH), rhs, (((1,), (1,)), ((), ())),
            preferred_element_type=F32,
        )
        for k, zz in enumerate((za, zb)):
            gap = rsq[...] + csv[pl.ds(zz, 1), :] - 2.0 * inner[:, k * CHUNK : (k + 1) * CHUNK]
            lane = pl.ds(pl.multiple_of(zz * CHUNK, CHUNK), CHUNK)
            logits[:, lane] = -jnp.sqrt(jnp.maximum(gap, 1.0)) * INV_SCALE

    def column_stats(zz):
        lane = pl.ds(pl.multiple_of(zz * CHUNK, CHUNK), CHUNK)
        block = logits[:, lane]
        peak = jnp.max(block, axis=0, keepdims=True)
        total = jnp.sum(jnp.exp(block - peak), axis=0, keepdims=True)
        cstat[z * NC + c, pl.ds(zz, 1), :] = peak + jnp.log(total)

    tile(zmod(-1), zmod(1))
    column_stats(zmod(-1))
    column_stats(zmod(1))
    z_arrive(3, 1)
    tile(zmod(-2), zmod(2))
    column_stats(zmod(-2))
    column_stats(zmod(2))
    sib_arrive(3)
    col_squares(zmod(-3))
    col_squares(zmod(3))
    tile(zmod(-3), zmod(3))
    column_stats(zmod(-3))
    column_stats(zmod(3))
    z_arrive(4, 0)
    sib_arrive(4)
    col_squares(zmod(4))
    tile(z, zmod(4))
    mine_rows = pl.ds(pl.multiple_of(own * PER, PER), PER)
    mine_lanes = pl.ds(pl.multiple_of(z * CHUNK, CHUNK), CHUNK)
    block = logits[mine_rows, mine_lanes]
    lane_id = lax.broadcasted_iota(jnp.int32, block.shape, 1)
    row_id = lax.broadcasted_iota(jnp.int32, block.shape, 0)
    logits[mine_rows, mine_lanes] = jnp.where(lane_id == row_id + c * 64, MASKED, block)
    column_stats(z)
    column_stats(zmod(4))

    def exchange(buf, me, peer_of, k):
        def one(t, carry):
            there = lax.rem(me + t, 16)
            pltpu.make_async_remote_copy(
                src_ref=buf.at[me], dst_ref=buf.at[me], send_sem=xs.at[k], recv_sem=xr.at[k],
                device_id=peer_of(there), device_id_type=pl.DeviceIdType.MESH,
            ).start()
            return carry
        lax.fori_loop(1, 16, one, 0)

    def exchanged(buf, k):
        some = buf.at[pl.ds(0, 15)]
        pltpu.make_async_copy(some, some, xr.at[k]).wait()

    def z_peer(k):
        return {"z": k // 2, "y": y, "c": lax.rem(k, 2), "x": x}

    def pq_peer(k):
        return at_pq(lax.rem(k, 4), k // 4)

    zc = z * NC + c
    exchange(cstat, zc, z_peer, 0)

    def row_stats(k, carry):
        part = pl.ds(pl.multiple_of(k * 128, 128), 128)
        block = logits[part, :]
        peak = jnp.max(block, axis=1, keepdims=True)
        total = jnp.sum(jnp.exp(block - peak), axis=1, keepdims=True)
        rstat[own, pl.ds(k, 1), :] = to_lanes(peak + jnp.log(total))
        return carry

    lax.fori_loop(0, 4, row_stats, 0)
    exchange(rstat, own, pq_peer, 1)

    def joined(buf):
        peak = buf[0]
        for k in range(1, 16):
            peak = jnp.maximum(peak, buf[k])
        total = jnp.exp(buf[0] - peak)
        for k in range(1, 16):
            total = total + jnp.exp(buf[k] - peak)
        return peak + jnp.log(total)

    exchanged(cstat, 0)
    csv[...] = 0.5 * joined(cstat)
    exchanged(rstat, 1)
    rall = 0.5 * joined(rstat)
    for k in range(4):
        rvec[pl.ds(k * 128, 128), :] = to_rows(rall[k : k + 1, :])
    is_real = lax.rem(lax.broadcasted_iota(jnp.int32, (1, COLS), 1) // PER, 2) == 1

    def halves(k, carry):
        part = pl.ds(pl.multiple_of(k * 128, 128), 128)
        shift = jnp.concatenate([csv[j : j + 1, :] for j in range(NZ)], axis=1)
        half = jnp.exp(logits[part, :] - rvec[part, :] - shift)
        logits[part, :] = half
        real = jnp.sum(jnp.where(is_real, half, 0.0), axis=1, keepdims=True)
        gen = jnp.sum(jnp.where(is_real, 0.0, half), axis=1, keepdims=True)
        mstat[own, pl.ds(k, 1), :] = to_lanes(gen)
        mstat[own, pl.ds(4 + k, 1), :] = to_lanes(real)
        return carry

    lax.fori_loop(0, 4, halves, 0)
    exchange(mstat, own, pq_peer, 2)
    exchanged(mstat, 2)
    mass = mstat[0]
    for k in range(1, 16):
        mass = mass + mstat[k]
    for k in range(4):
        gvec[pl.ds(k * 128, 128), :] = to_rows(mass[k : k + 1, :])
        mvec[pl.ds(k * 128, 128), :] = -to_rows(mass[k + 4 : k + 5, :])

    def drift(qq):
        part = pl.ds(pl.multiple_of(qq * 128, 128), 128)
        scale = jnp.where(is_real, gvec[part, :], mvec[part, :])
        weights = (logits[part, :] * scale).astype(BF16)
        return jnp.dot(weights, cols[...].reshape(COLS, WIDTH), preferred_element_type=F32)

    ahead, behind = at_pq(p, after), at_pq(p, before)
    part = drift(across).reshape(4, PER, WIDTH)
    psend[across] = part.astype(BF16)
    send(psend.at[across, pl.ds(0, 2)], far1.at[0], fs.at[0], fr.at[0], ahead)
    send(psend.at[across, pl.ds(2, 2)], far1.at[1], fs.at[1], fr.at[1], behind)
    part = drift(after).reshape(4, PER, WIDTH)
    psend[after, 2:4] = part[2:4].astype(BF16)
    send(psend.at[after, pl.ds(2, 2)], near1.at[0, pl.ds(2, 2)], fs.at[2], fr.at[2], ahead)
    acc[0:2] = part[0:2]
    part = drift(before).reshape(4, PER, WIDTH)
    psend[before, 0:2] = part[0:2].astype(BF16)
    send(psend.at[before, pl.ds(0, 2)], near1.at[1, pl.ds(0, 2)], fs.at[3], fr.at[3], behind)
    acc[2:4] = part[2:4]
    arrived(far1.at[0], fr.at[0])
    psend[after, 0:2] = (acc[0:2] + far1[0].astype(F32)).astype(BF16)
    send(psend.at[after, pl.ds(0, 2)], near1.at[0, pl.ds(0, 2)], fs.at[4], fr.at[4], ahead)
    arrived(far1.at[1], fr.at[1])
    psend[before, 2:4] = (acc[2:4] + far1[1].astype(F32)).astype(BF16)
    send(psend.at[before, pl.ds(2, 2)], near1.at[1, pl.ds(2, 2)], fs.at[5], fr.at[5], behind)
    acc[...] = drift(q).reshape(4, PER, WIDTH)
    arrived(near1.at[0, pl.ds(2, 2)], fr.at[2])
    arrived(near1.at[1, pl.ds(0, 2)], fr.at[3])
    arrived(near1.at[0, pl.ds(0, 2)], fr.at[4])
    arrived(near1.at[1, pl.ds(2, 2)], fr.at[5])

    def summed(k):
        return acc[k] + near1[0, k].astype(F32) + near1[1, k].astype(F32)

    ahead, behind = at_pq(pmod(1), q), at_pq(pmod(-1), q)
    qsend[2] = summed(pmod(2)).astype(BF16)
    send(qsend.at[2, pl.ds(0, 16)], far2.at[0], fs.at[6], fr.at[6], ahead)
    send(qsend.at[2, pl.ds(16, 16)], far2.at[1], fs.at[7], fr.at[7], behind)
    part = summed(pmod(1))
    qsend[1, 16:32] = part[16:32].astype(BF16)
    send(qsend.at[1, pl.ds(16, 16)], near2.at[0, pl.ds(16, 16)], fs.at[8], fr.at[8], ahead)
    hold_a = part[0:16]
    part = summed(pmod(-1))
    qsend[3, 0:16] = part[0:16].astype(BF16)
    send(qsend.at[3, pl.ds(0, 16)], near2.at[1, pl.ds(0, 16)], fs.at[9], fr.at[9], behind)
    hold_b = part[16:32]
    arrived(far2.at[0], fr.at[6])
    qsend[1, 0:16] = (hold_a + far2[0].astype(F32)).astype(BF16)
    send(qsend.at[1, pl.ds(0, 16)], near2.at[0, pl.ds(0, 16)], fs.at[10], fr.at[10], ahead)
    arrived(far2.at[1], fr.at[7])
    qsend[3, 16:32] = (hold_b + far2[1].astype(F32)).astype(BF16)
    send(qsend.at[3, pl.ds(16, 16)], near2.at[1, pl.ds(16, 16)], fs.at[11], fr.at[11], behind)
    raw = summed(p)
    arrived(near2.at[0, pl.ds(16, 16)], fr.at[8])
    arrived(near2.at[1, pl.ds(0, 16)], fr.at[9])
    arrived(near2.at[0, pl.ds(0, 16)], fr.at[10])
    arrived(near2.at[1, pl.ds(16, 16)], fr.at[11])
    raw = raw + near2[0].astype(F32) + near2[1].astype(F32)
    out_ref[...] = raw
    n1[zc] = jnp.broadcast_to(jnp.sum(raw * raw, keepdims=True), (8, 128))
    exchange(n1, zc, z_peer, 3)
    exchanged(n1, 3)
    total = n1[0]
    for k in range(1, 16):
        total = total + n1[k]
    n2[own] = total
    exchange(n2, own, pq_peer, 4)
    exchanged(n2, 4)
    total = n2[0]
    for k in range(1, 16):
        total = total + n2[k]
    scale = lax.rsqrt(total[0:1, 0:1] / (NX * NY * NZ * NC * PER * WIDTH) + EPS)
    out_ref[...] = out_ref[...] * scale

    for copy in pending:
        copy.wait_send()
    for k, buf in enumerate((cstat, rstat, mstat, n1, n2)):
        some = buf.at[pl.ds(0, 15)]
        pltpu.make_async_copy(some, some, xs.at[k]).wait()


def on_device(gen, real):
    dma = pltpu.SemaphoreType.DMA
    return pl.pallas_call(
        kernel,
        out_shape=jax.ShapeDtypeStruct((PER, WIDTH), F32),
        in_specs=[pl.BlockSpec(memory_space=pl.ANY)] * 2,
        out_specs=pl.BlockSpec(memory_space=pltpu.VMEM),
        scratch_shapes=[
            pltpu.VMEM((16, PER, WIDTH), BF16),
            pltpu.VMEM((NZ, NC, 2, PER, WIDTH), BF16),
            pltpu.VMEM((ROWS, COLS), F32),
            pltpu.VMEM((8, 128), BF16),
            pltpu.VMEM((ROWS, 1), F32),
            pltpu.VMEM((ROWS, 1), F32),
            pltpu.VMEM((ROWS, 1), F32),
            pltpu.VMEM((ROWS, 1), F32),
            pltpu.VMEM((NZ, CHUNK), F32),
            pltpu.VMEM((16, NZ, CHUNK), F32),
            pltpu.VMEM((16, 4, 128), F32),
            pltpu.VMEM((16, 8, 128), F32),
            pltpu.VMEM((16, 8, 128), F32),
            pltpu.VMEM((16, 8, 128), F32),
            pltpu.VMEM((4, 4, PER, WIDTH), BF16),
            pltpu.VMEM((4, PER, WIDTH), F32),
            pltpu.VMEM((2, 2, PER, WIDTH), BF16),
            pltpu.VMEM((2, 4, PER, WIDTH), BF16),
            pltpu.VMEM((4, PER, WIDTH), BF16),
            pltpu.VMEM((2, PER // 2, WIDTH), BF16),
            pltpu.VMEM((2, PER, WIDTH), BF16),
            dma((3,)), dma((16,)), dma((16,)), dma((20,)), dma((20,)),
            dma((8,)), dma((8,)), dma((5,)), dma((5,)), dma((12,)), dma((12,)),
        ],
        compiler_params=pltpu.CompilerParams(
            collective_id=0, has_side_effects=True, vmem_limit_bytes=60 * 1024 * 1024
        ),
    )(gen, real)


def solution(mesh):
    torus = Mesh(mesh.devices.reshape(NZ, NY, NC, NX), AXES)
    return jax.shard_map(
        on_device,
        mesh=torus,
        in_specs=(P(AXES, None), P(AXES, None)),
        out_specs=P(AXES, None),
        check_vma=False,
    )
```

time: 255 us -> 85.8 us (0.34)
  blocking collectives: 101 us -> 0 us
  waiting for transfers between devices: 98.2 us -> 0 us
  Pallas kernels: 0 us -> 84 us
  other arithmetic: 17.1 us -> 0 us
  matrix products: 14.6 us -> 0 us
  between operations: 14.2 us -> 0.01 us
  starting transfers between devices: 4.83 us -> 0 us
  local copies, waits for them, and re-layouts: 4.99 us -> 1.67 us
    all_gather x1 -> x0, waiting for transfers between devices: 91 us -> none  [side_by_side(): lax.all_gather(both, axis, axis=dim, tiled=True)]
    pallas_call x0 -> x1, Pallas kernels: none -> 84 us  [on_device(): pl.pallas_call(kernel, out_shape=jax.ShapeDtypeStruct((PER, WIDTH), F32),...]
    all_gather x3 -> x0, blocking collectives: 38.6 us -> none  [all_in_one(): both, at, found = (lax.all_gather(jnp.concatenate(lines), axis), 0, {})]
    psum x4 -> x0, blocking collectives: 38.2 us -> none  [over_axes(): return functools.reduce(lax.psum, axes, value)]
    all_to_all x2 -> x0, blocking collectives: 23.8 us -> none  [the longest x1 15.8 us: sent_and_summed(): lax.all_to_all(tiles, axis, split_axis=0, concat_axis=0, tiled=True)]
    dot_general x4 -> x0, matrix products: 14.6 us -> none  [the longest x2 5.2 us: distance_logits(): jnp.einsum('rd,kd->rk', row_feats, target_feature_vectors, preferred_elem...]
    reduce_sum x7 -> x0, other arithmetic: 12.3 us -> none  [the longest x2 8.11 us: squares(): return jnp.sum(jnp.square(values.astype(jnp.float32)), axis=1)]
    all_to_all x1 -> x0, waiting for transfers between devices: 7.15 us -> none  [from_everyone(): lax.all_to_all(jnp.broadcast_to(value[None], (length, *value.shape)), axi...]
  transfers between devices with their start and end apart: 2 -> 0, of which waited for: 2 -> 0; matrix products, arithmetic and copies ran while one was open for 1% -> 0% of each run, Pallas kernels for 0% -> 0%
where the time goes in v1:
time: 85.8 us; the launch traced here: 85.7 us
  Pallas kernels  84 us (98%)
  local copies, waits for them, and re-layouts  1.67 us (2%)
    pallas_call x1, Pallas kernels, on_device(): pl.pallas_call(kernel, out_shape=jax.ShapeDtypeStruct((PER, WIDTH), F32),...  84 us

profile of v1, /device:TPU:1, one launch (start us, length us, event | category | flops | bytes accessed | tf_op | source)
XLA Modules:
  0.0 85.7 jit_solution(5177285858428558525)
XLA Ops:
  0.0 84.0 %shard_map.28 = f32[32,2048]{1,0:T(8,128)} custom-call(bf16[32,2048]{1,0:T(8,128)(2,1)} %gen_ref.1, bf16[32,2048]{1,0:T(8,128)(2,1)} %real_ref.1), custom_call_target="tpu_custom_call" | custom-call | tf_op jit(solution)/shard_map/pallas_call | solution.py:395
  84.0 1.7 %copy.4 = f32[32,2048]{1,0:T(8,128)} copy(f32[32,2048]{1,0:T(8,128)} %shard_map.28) | data formatting | bytes 524288

commit v2 on v1

v2 whole, which is shorter than its diff:
```python
import jax
import jax.numpy as jnp
from jax import lax
from jax.experimental import pallas as pl
from jax.experimental.pallas import tpu as pltpu
from jax.sharding import Mesh
from jax.sharding import PartitionSpec as P

AXES = ("z", "y", "c", "x")
NZ, NY, NC, NX = 8, 4, 2, 4
PER = 32
HALF = PER // 2
WIDTH = 2048
ROWS = NX * NY * PER
CHUNK = 2 * NC * PER
COLS = NZ * CHUNK
SLICES = 4
PIECE = WIDTH // SLICES
INV_SCALE = 1.0 / 0.3
MASKED = -1e30
EPS = 1e-6
F32 = jnp.float32
BF16 = jnp.bfloat16
MESH = pl.DeviceIdType.MESH
SEMS = 128


def eye():
    return lax.broadcasted_iota(jnp.int32, (128, 128), 0) == lax.broadcasted_iota(
        jnp.int32, (128, 128), 1
    )


def to_lanes(v):
    return jnp.sum(jnp.where(eye(), jnp.broadcast_to(v, (128, 128)), 0.0), axis=0, keepdims=True)


def to_rows(v):
    return jnp.sum(jnp.where(eye(), jnp.broadcast_to(v, (128, 128)), 0.0), axis=1, keepdims=True)


def kernel(
    gen_ref, real_ref, raw_ref, norm_ref,
    rows, cols, logits, rsq, rvec, csq, cown, raw,
    cstat, rstat, mstat, n1, n2,
    weights, psend, acc, kept, far, near, qsend, qrecv,
    in_sem, out_sem, ssem, rsem, xs, xr,
):
    z, y, c, x = (lax.axis_index(a) for a in AXES)
    p = x * (1 - c) + y * c
    q = y * (1 - c) + x * c

    def at_z(zz, cc=c):
        return {"z": zz, "y": y, "c": cc, "x": x}

    def at_pq(pp, qq):
        return {"z": z, "y": qq * (1 - c) + pp * c, "c": c, "x": pp * (1 - c) + qq * c}

    def zmod(d):
        return lax.rem(z + (d + NZ), NZ)

    def pmod(d):
        return lax.rem(p + (d + 4), 4)

    def qmod(d):
        return lax.rem(q + (d + 4), 4)

    sibling = at_z(z, 1 - c)
    pending, used, index = [], [], {}

    def drain():
        for copy in pending:
            copy.wait_send()
        for k, buf in used:
            some = buf.at[pl.ds(0, 15)]
            pltpu.make_async_copy(some, some, xs.at[k]).wait()

    def send(key, src, dst, dev):
        k = index.setdefault(key, len(index))
        assert k == len(index) - 1 and k < SEMS
        copy = pltpu.make_async_remote_copy(
            src_ref=src, dst_ref=dst, send_sem=ssem.at[k], recv_sem=rsem.at[k],
            device_id=dev, device_id_type=MESH,
        )
        copy.start()
        pending.append(copy)

    def arrived(key, ref):
        pltpu.make_async_copy(ref, ref, rsem.at[index[key]]).wait()

    own = q * 4 + p
    loads = (
        pltpu.make_async_copy(gen_ref, rows.at[own], in_sem.at[0]),
        pltpu.make_async_copy(gen_ref, cols.at[z, c, 0], in_sem.at[1]),
        pltpu.make_async_copy(real_ref, cols.at[z, c, 1], in_sem.at[2]),
    )
    for copy in loads:
        copy.start()
    barrier = pltpu.get_barrier_semaphore()
    around = (
        sibling, at_z(zmod(1)), at_z(zmod(-1)),
        at_pq(pmod(1), q), at_pq(pmod(-1), q), at_pq(p, qmod(1)), at_pq(p, qmod(-1)),
    )
    for dev in around:
        pl.semaphore_signal(barrier, inc=1, device_id=dev, device_id_type=MESH)
    pl.semaphore_wait(barrier, len(around))
    for copy in loads:
        copy.wait()

    top, low = pl.ds(0, HALF), pl.ds(HALF, HALF)

    def z_piece(d, h, j):
        kind = j // 2 if d == 0 else 1 - j // 2
        return cols.at[zmod((2 * d - 1) * h), c, kind, low if j % 2 else top], kind

    def z_send(d, h, j):
        src, _ = z_piece(d, h - 1, j)
        send(("z", d, h, j), src, src, at_z(zmod(1 - 2 * d)))

    def z_arrive(h, j):
        for d in (0, 1):
            src, kind = z_piece(d, h, j)
            arrived(("z", d, h, j), src)
            if h < 3 or (h == 3 and j < 2):
                z_send(d, h + 1, j)
            if h == 4:
                send(("s", d, h, j), src, src, sibling)
            elif j % 2:
                whole = cols.at[zmod((2 * d - 1) * h), c, kind]
                send(("s", d, h, kind), whole, whole, sibling)

    def sib_arrive(h):
        for d in (0, 1):
            zz = zmod((2 * d - 1) * h)
            if h == 4:
                for j in (0, 1):
                    arrived(("s", d, h, j), cols.at[zz, 1 - c, d, low if j else top])
            elif h or not d:
                for kind in (0, 1):
                    arrived(("s", d, h, kind), cols.at[zz, 1 - c, kind])

    def at_row(dq, dp):
        return qmod(dq) * 4 + pmod(dp)

    def q_sends(dp):
        block = rows.at[at_row(0, dp)]
        send(("q", 1, dp), block, block, at_pq(p, qmod(1)))
        send(("q", -1, dp), block, block, at_pq(p, qmod(-1)))

    def p_arrive(d):
        arrived(("p", d), rows.at[at_row(0, -d)])
        half = rows.at[at_row(0, -d), top if d > 0 else low]
        send(("pf", d), half, half, at_pq(pmod(d), q))
        q_sends(-d)

    def p_far():
        arrived(("pf", 1), rows.at[at_row(0, 2), top])
        arrived(("pf", -1), rows.at[at_row(0, 2), low])
        q_sends(2)

    def q_arrive(dp):
        for d in (1, -1):
            arrived(("q", d, dp), rows.at[at_row(-d, dp)])
            half = rows.at[at_row(-d, dp), top if d > 0 else low]
            send(("qf", d, dp), half, half, at_pq(p, qmod(d)))

    def q_far(dp):
        arrived(("qf", 1, dp), rows.at[at_row(2, dp), top])
        arrived(("qf", -1, dp), rows.at[at_row(2, dp), low])

    def squares_of(value):
        value = value.astype(F32)
        return jnp.sum(value * value, axis=1, keepdims=True)

    def row_squares(dq):
        def one(k, carry):
            g = qmod(dq) * 4 + k
            rsq[pl.ds(g * PER, PER), :] = jnp.broadcast_to(squares_of(rows[g]), (PER, CHUNK))
            return carry
        lax.fori_loop(0, 4, one, 0)

    def col_squares(d):
        csq[pl.ds(zmod(d), 1), :] = to_lanes(squares_of(cols[zmod(d)].reshape(CHUNK, WIDTH)))

    def lanes_of(d):
        return pl.ds(pl.multiple_of(zmod(d) * CHUNK, CHUNK), CHUNK)

    zc = z * NC + c

    def tile(*ds):
        rhs = [cols[zmod(d)].reshape(CHUNK, WIDTH) for d in ds]
        rhs = jnp.concatenate(rhs, axis=0) if len(rhs) > 1 else rhs[0]
        inner = lax.dot_general(
            rows[...].reshape(ROWS, WIDTH), rhs, (((1,), (1,)), ((), ())),
            preferred_element_type=F32,
        )
        for k, d in enumerate(ds):
            gap = rsq[...] + csq[pl.ds(zmod(d), 1), :] - 2.0 * inner[:, k * CHUNK : (k + 1) * CHUNK]
            gap = jnp.maximum(gap, 1.0)
            logits[:, lanes_of(d)] = gap * lax.rsqrt(gap) * -INV_SCALE
        if ds == (0,):
            mine = pl.ds(pl.multiple_of(own * PER, PER), PER)
            block = logits[mine, lanes_of(0)]
            lane_id = lax.broadcasted_iota(jnp.int32, block.shape, 1)
            row_id = lax.broadcasted_iota(jnp.int32, block.shape, 0)
            logits[mine, lanes_of(0)] = jnp.where(lane_id == row_id + c * 2 * PER, MASKED, block)
        for d in ds:
            block = logits[:, lanes_of(d)]
            peak = jnp.max(block, axis=0, keepdims=True)
            total = jnp.sum(jnp.exp(block - peak), axis=0, keepdims=True)
            cstat[zc, pl.ds(zmod(d), 1), :] = peak + jnp.log(total)

    for j in range(4):
        for d in (0, 1):
            z_send(d, 1, j)
    for d in (1, -1):
        send(("p", d), rows.at[own], rows.at[own], at_pq(pmod(d), q))
    q_sends(0)
    for kind in (0, 1):
        send(("s", 0, 0, kind), cols.at[z, c, kind], cols.at[z, c, kind], sibling)

    events = []

    def plan(when, what, *args):
        events.append((when, len(events), what, args))

    for h in range(1, 5):
        for j in range(4 if h < 4 else 2):
            plan(3.0 + 1.4 * ((h - 1) * 4 + j + 1), z_arrive, h, j)
    plan(4.3, p_arrive, 1)
    plan(4.3, p_arrive, -1)
    plan(5.9, q_arrive, 0)
    plan(8.1, p_far)
    plan(9.2, q_arrive, -1)
    plan(10.2, q_arrive, 1)
    plan(12.5, q_arrive, 2)
    plan(9.9, q_far, 0)
    plan(13.0, q_far, -1)
    plan(14.0, q_far, 1)
    plan(16.3, q_far, 2)
    plan(6.0, sib_arrive, 0)
    plan(6.0, col_squares, 0)
    plan(8.2, row_squares, 0)
    plan(12.6, sib_arrive, 1)
    plan(12.6, col_squares, 1)
    plan(13.1, col_squares, -1)
    plan(14.3, row_squares, 1)
    plan(14.6, row_squares, -1)
    plan(16.4, row_squares, 2)
    plan(16.5, tile, 0)
    plan(17.1, tile, 1, -1)
    plan(18.5, sib_arrive, 2)
    plan(18.5, col_squares, 2)
    plan(18.6, col_squares, -2)
    plan(19.9, tile, 2, -2)
    plan(22.61, sib_arrive, 3)
    plan(22.62, col_squares, 3)
    plan(22.63, col_squares, -3)
    plan(22.64, tile, 3, -3)
    for _, _, what, args in sorted(events, key=lambda e: e[:2]):
        what(*args)
    sib_arrive(4)
    col_squares(4)
    tile(4)

    z_order = [(d, k) for d in (4, 3, -3, 2, -2, 1, -1, 0) for k in (1, 0) if d or k]
    pq_order = sorted(
        ((i, j) for i in range(4) for j in range(4) if i or j),
        key=lambda d: -min(d[0], 4 - d[0]) - min(d[1], 4 - d[1]),
    )
    z_peers = [at_z(zmod(d), c + k - 2 * c * k) for d, k in z_order]
    pq_peers = [at_pq(pmod(i), qmod(j)) for i, j in pq_order]

    def exchange(buf, me, peers):
        k = len(used)
        for dev in peers:
            pltpu.make_async_remote_copy(
                src_ref=buf.at[me], dst_ref=buf.at[me], send_sem=xs.at[k], recv_sem=xr.at[k],
                device_id=dev, device_id_type=MESH,
            ).start()
        used.append((k, buf))

        def wait():
            some = buf.at[pl.ds(0, 15)]
            pltpu.make_async_copy(some, some, xr.at[k]).wait()

        return wait

    def joined(buf):
        peak = buf[0]
        for k in range(1, 16):
            peak = jnp.maximum(peak, buf[k])
        total = jnp.exp(buf[0] - peak)
        for k in range(1, 16):
            total = total + jnp.exp(buf[k] - peak)
        return peak + jnp.log(total)

    def in_line(v):
        return jnp.concatenate([v[j : j + 1, :] for j in range(NZ)], axis=1)

    columns_known = exchange(cstat, zc, z_peers)
    cown[...] = cstat[zc]

    def row_stats(k, carry):
        part = pl.ds(pl.multiple_of(k * 128, 128), 128)
        block = logits[part, :]
        peak = jnp.max(block, axis=1, keepdims=True)
        total = peak + jnp.log(jnp.sum(jnp.exp(block - peak), axis=1, keepdims=True))
        rvec[part, :] = 0.5 * total
        rstat[own, pl.ds(k, 1), :] = to_lanes(total)
        return carry

    lax.fori_loop(0, 4, row_stats, 0)
    rows_known = exchange(rstat, own, pq_peers)

    def start_halves(k, carry):
        part = pl.ds(pl.multiple_of(k * 128, 128), 128)
        logits[part, :] = jnp.exp(logits[part, :] - rvec[part, :] - 0.5 * in_line(cown[...]))
        return carry

    lax.fori_loop(0, 4, start_halves, 0)
    columns_known()
    cown[...] = jnp.exp(0.5 * (cown[...] - joined(cstat)))
    lane_id = lax.broadcasted_iota(jnp.int32, (1, CHUNK), 1)
    is_real = lax.rem(lane_id // PER, 2) == 1

    def masses(k, carry):
        part = pl.ds(pl.multiple_of(k * 128, 128), 128)
        total = logits[part, 0:CHUNK] * cown[0:1, :]
        for j in range(1, NZ):
            total = total + logits[part, j * CHUNK : (j + 1) * CHUNK] * cown[j : j + 1, :]
        real = jnp.sum(jnp.where(is_real, total, 0.0), axis=1, keepdims=True)
        gen = jnp.sum(jnp.where(is_real, 0.0, total), axis=1, keepdims=True)
        mstat[own, pl.ds(k, 1), :] = to_lanes(gen)
        mstat[own, pl.ds(4 + k, 1), :] = to_lanes(real)
        return carry

    lax.fori_loop(0, 4, masses, 0)
    masses_known = exchange(mstat, own, pq_peers)
    rows_known()
    joint = joined(rstat)
    shares = [jnp.exp(0.5 * (rstat[k] - joint)) for k in range(16)]
    my_share = jnp.exp(0.5 * (rstat[own] - joint))
    masses_known()
    gen = shares[0] * mstat[0, 0:4]
    real = shares[0] * mstat[0, 4:8]
    for k in range(1, 16):
        gen = gen + shares[k] * mstat[k, 0:4]
        real = real + shares[k] * mstat[k, 4:8]
    mstat[16, 0:4] = my_share * gen
    mstat[16, 4:8] = -my_share * real

    def weigh(qq, at):
        part = pl.ds(pl.multiple_of(qq * 128, 128), 128)
        on_real = to_rows(mstat[16, pl.ds(qq, 1), :])
        on_gen = to_rows(mstat[16, pl.ds(qq + 4, 1), :])
        scale = jnp.where(is_real, on_real, on_gen)
        for j in range(NZ):
            half = logits[part, j * CHUNK : (j + 1) * CHUNK] * cown[j : j + 1, :]
            weights[at, :, j * CHUNK : (j + 1) * CHUNK] = (half * scale).astype(BF16)

    def drift(w, s):
        samples = cols[:, :, :, :, s * PIECE : (s + 1) * PIECE].reshape(COLS, PIECE)
        return jnp.dot(w, samples, preferred_element_type=F32)

    before, after, across = qmod(-1), qmod(1), qmod(2)
    ahead, behind = at_pq(p, after), at_pq(p, before)
    lo, hi = pl.ds(0, 2), pl.ds(2, 2)
    weigh(across, 0)
    for s in range(SLICES):
        psend[s, 0] = drift(weights[0], s).reshape(4, PER, PIECE).astype(BF16)
        send(("f", 1, s), psend.at[s, 0, lo], far.at[s, 0], ahead)
        send(("f", -1, s), psend.at[s, 0, hi], far.at[s, 1], behind)
    weigh(after, 1)
    weigh(before, 2)
    for s in range(SLICES):
        part = drift(weights[1:3].reshape(256, COLS), s).reshape(8, PER, PIECE)
        psend[s, 1, 2:4] = part[2:4].astype(BF16)
        send(("i", 1, s), psend.at[s, 1, hi], near.at[s, 0, hi], ahead)
        psend[s, 2, 0:2] = part[4:6].astype(BF16)
        send(("i", -1, s), psend.at[s, 2, lo], near.at[s, 1, lo], behind)
        kept[s, 0:2] = part[0:2]
        kept[s, 2:4] = part[6:8]
    weigh(q, 0)
    for s in range(SLICES):
        acc[s] = drift(weights[0], s).reshape(4, PER, PIECE)
    for s in range(SLICES):
        arrived(("f", 1, s), far.at[s, 0])
        psend[s, 1, 0:2] = (kept[s, 0:2] + far[s, 0].astype(F32)).astype(BF16)
        send(("d", 1, s), psend.at[s, 1, lo], near.at[s, 0, lo], ahead)
        arrived(("f", -1, s), far.at[s, 1])
        psend[s, 2, 2:4] = (kept[s, 2:4] + far[s, 1].astype(F32)).astype(BF16)
        send(("d", -1, s), psend.at[s, 2, hi], near.at[s, 1, hi], behind)
    for s in range(SLICES):
        arrived(("i", 1, s), near.at[s, 0, hi])
        arrived(("i", -1, s), near.at[s, 1, lo])
        arrived(("d", 1, s), near.at[s, 0, lo])
        arrived(("d", -1, s), near.at[s, 1, hi])
        for d in (2, 1, 3):
            k = pmod(d)
            total = acc[s, k] + near[s, 0, k].astype(F32) + near[s, 1, k].astype(F32)
            qsend[s, d - 1] = total.astype(BF16)
            send(("r", d, s), qsend.at[s, d - 1], qrecv.at[s, d - 1], at_pq(k, q))
    square = jnp.zeros((PER, 128), F32)
    for s in range(SLICES):
        total = acc[s, p] + near[s, 0, p].astype(F32) + near[s, 1, p].astype(F32)
        for d in (1, 3, 2):
            arrived(("r", d, s), qrecv.at[s, d - 1])
            total = total + qrecv[s, d - 1].astype(F32)
        raw[:, s * PIECE : (s + 1) * PIECE] = total
        for k in range(PIECE // 128):
            lane = total[:, k * 128 : (k + 1) * 128]
            square = square + lane * lane
    n1[zc] = jnp.broadcast_to(jnp.sum(square, keepdims=True), (1, 128))
    first_known = exchange(n1, zc, z_peers)
    out = pltpu.make_async_copy(raw, raw_ref, out_sem)
    out.start()
    first_known()
    total = n1[0]
    for k in range(1, 16):
        total = total + n1[k]
    n2[own] = total
    second_known = exchange(n2, own, pq_peers)
    out.wait()
    second_known()
    total = n2[0]
    for k in range(1, 16):
        total = total + n2[k]
    count = NX * NY * NZ * NC * PER * WIDTH
    norm_ref[0, 0] = lax.rsqrt(total / count + EPS)[0, 0]
    drain()


def on_device(gen, real):
    dma = pltpu.SemaphoreType.DMA
    raw, norm = pl.pallas_call(
        kernel,
        out_shape=(
            jax.ShapeDtypeStruct((PER, WIDTH), F32), jax.ShapeDtypeStruct((1, 1), F32),
        ),
        in_specs=[pl.BlockSpec(memory_space=pl.ANY)] * 2,
        out_specs=(
            pl.BlockSpec(memory_space=pl.ANY), pl.BlockSpec(memory_space=pltpu.SMEM),
        ),
        scratch_shapes=[
            pltpu.VMEM((16, PER, WIDTH), BF16),
            pltpu.VMEM((NZ, NC, 2, PER, WIDTH), BF16),
            pltpu.VMEM((ROWS, COLS), F32),
            pltpu.VMEM((ROWS, CHUNK), F32),
            pltpu.VMEM((ROWS, 1), F32),
            pltpu.VMEM((NZ, CHUNK), F32),
            pltpu.VMEM((NZ, CHUNK), F32),
            pltpu.VMEM((PER, WIDTH), F32),
            pltpu.VMEM((16, NZ, CHUNK), F32),
            pltpu.VMEM((16, 4, 128), F32),
            pltpu.VMEM((17, 8, 128), F32),
            pltpu.VMEM((16, 1, 128), F32),
            pltpu.VMEM((16, 1, 128), F32),
            pltpu.VMEM((3, 128, COLS), BF16),
            pltpu.VMEM((SLICES, 3, 4, PER, PIECE), BF16),
            pltpu.VMEM((SLICES, 4, PER, PIECE), F32),
            pltpu.VMEM((SLICES, 4, PER, PIECE), F32),
            pltpu.VMEM((SLICES, 2, 2, PER, PIECE), BF16),
            pltpu.VMEM((SLICES, 2, 4, PER, PIECE), BF16),
            pltpu.VMEM((SLICES, 3, PER, PIECE), BF16),
            pltpu.VMEM((SLICES, 3, PER, PIECE), BF16),
            dma((3,)), dma, dma((SEMS,)), dma((SEMS,)), dma((5,)), dma((5,)),
        ],
        compiler_params=pltpu.CompilerParams(
            collective_id=0, has_side_effects=True, vmem_limit_bytes=60 * 1024 * 1024
        ),
    )(gen, real)
    return raw * norm


def solution(mesh):
    torus = Mesh(mesh.devices.reshape(NZ, NY, NC, NX), AXES)
    return jax.shard_map(
        on_device,
        mesh=torus,
        in_specs=(P(AXES, None), P(AXES, None)),
        out_specs=P(AXES, None),
        check_vma=False,
    )
```

time: 85.8 us -> 77.4 us (0.902)
  Pallas kernels: 84 us -> 74.9 us
  other arithmetic: 0 us -> 2.31 us
  local copies, waits for them, and re-layouts: 1.67 us -> 0 us
    pallas_call x1, Pallas kernels: 84 us -> 74.9 us  [on_device(): pl.pallas_call(kernel, out_shape=(jax.ShapeDtypeStruct((PER, WIDTH), F32)...]
    mul x0 -> x1, other arithmetic: none -> 2.31 us  [on_device(): return raw * norm]
    unnamed x1 -> x0, local copies, waits for them, and re-layouts: 1.67 us -> none
where the time goes in v2:
time: 77.4 us; the launch traced here: 77.2 us
  Pallas kernels  74.9 us (97%)
  other arithmetic  2.31 us (3%)
    pallas_call x1, Pallas kernels, on_device(): pl.pallas_call(kernel, out_shape=(jax.ShapeDtypeStruct((PER, WIDTH), F32)...  74.9 us
    mul x1, other arithmetic, on_device(): return raw * norm  2.31 us

profile of v2, /device:TPU:1, one launch (start us, length us, event | category | flops | bytes accessed | tf_op | source)
XLA Modules:
  0.0 77.2 jit_solution(16192110703213408173)
XLA Ops:
  0.0 74.9 %shard_map.28 = (f32[32,2048]{1,0:T(8,128)}, f32[1,1]{1,0:T(1,128)}) custom-call(bf16[32,2048]{1,0:T(8,128)(2,1)} %gen_ref.1, bf16[32,2048]{1,0:T(8,128)(2,1)} %real_ref.1), custom_call_target="tpu_custom_call" | custom-call | tf_op jit(solution)/shard_map/pallas_call | solution.py:436
  74.9 2.3 %broadcast_multiply_fusion = f32[32,2048]{1,0:T(8,128)} fusion(f32[32,2048]{1,0:T(8,128)} %get-tuple-element.7, f32[]{:T(128)} %bitcast), kind=kLoop, calls=%fused_computation | loop fusion | flops 65536 | bytes 524292 | tf_op jit(solution)/shard_map/mul | solution.py:473

commit v3 on v2

--- a/solution.py
+++ b/solution.py
@@ -22,7 +22,7 @@
 F32 = jnp.float32
 BF16 = jnp.bfloat16
 MESH = pl.DeviceIdType.MESH
-SEMS = 128
+SEMS = 104
 
 
 def eye():
@@ -40,11 +40,11 @@
 
 
 def kernel(
-    gen_ref, real_ref, raw_ref, norm_ref,
-    rows, cols, logits, rsq, rvec, csq, cown, raw,
+    gen_ref, real_ref, out_ref,
+    rows, cols, logits, rsq, rvec, csq, cown,
     cstat, rstat, mstat, n1, n2,
     weights, psend, acc, kept, far, near, qsend, qrecv,
-    in_sem, out_sem, ssem, rsem, xs, xr,
+    in_sem, ssem, rsem, xs, xr,
 ):
     z, y, c, x = (lax.axis_index(a) for a in AXES)
     p = x * (1 - c) + y * c
@@ -66,11 +66,13 @@
         return lax.rem(q + (d + 4), 4)
 
     sibling = at_z(z, 1 - c)
-    pending, used, index = [], [], {}
+    used, index = [], {}
+    kinds = ("z", "s", "p", "f", "r")
 
     def drain():
-        for copy in pending:
-            copy.wait_send()
+        sent = (cols.at[pl.ds(0, 7), 0], cols.at[pl.ds(0, 8), 0], rows.at[pl.ds(0, 15)], psend, qsend)
+        for k, ref in enumerate(sent):
+            pltpu.make_async_copy(ref, ref, ssem.at[k]).wait()
         for k, buf in used:
             some = buf.at[pl.ds(0, 15)]
             pltpu.make_async_copy(some, some, xs.at[k]).wait()
@@ -78,12 +80,11 @@
     def send(key, src, dst, dev):
         k = index.setdefault(key, len(index))
         assert k == len(index) - 1 and k < SEMS
-        copy = pltpu.make_async_remote_copy(
-            src_ref=src, dst_ref=dst, send_sem=ssem.at[k], recv_sem=rsem.at[k],
+        kind = {"q": "p", "i": "f", "d": "f"}.get(key[0][0], key[0][0])
+        pltpu.make_async_remote_copy(
+            src_ref=src, dst_ref=dst, send_sem=ssem.at[kinds.index(kind)], recv_sem=rsem.at[k],
             device_id=dev, device_id_type=MESH,
-        )
-        copy.start()
-        pending.append(copy)
+        ).start()
 
     def arrived(key, ref):
         pltpu.make_async_copy(ref, ref, rsem.at[index[key]]).wait()
@@ -407,41 +408,34 @@
         for d in (1, 3, 2):
             arrived(("r", d, s), qrecv.at[s, d - 1])
             total = total + qrecv[s, d - 1].astype(F32)
-        raw[:, s * PIECE : (s + 1) * PIECE] = total
+        out_ref[:, s * PIECE : (s + 1) * PIECE] = total
         for k in range(PIECE // 128):
             lane = total[:, k * 128 : (k + 1) * 128]
             square = square + lane * lane
     n1[zc] = jnp.broadcast_to(jnp.sum(square, keepdims=True), (1, 128))
     first_known = exchange(n1, zc, z_peers)
-    out = pltpu.make_async_copy(raw, raw_ref, out_sem)
-    out.start()
     first_known()
     total = n1[0]
     for k in range(1, 16):
         total = total + n1[k]
     n2[own] = total
     second_known = exchange(n2, own, pq_peers)
-    out.wait()
     second_known()
     total = n2[0]
     for k in range(1, 16):
         total = total + n2[k]
     count = NX * NY * NZ * NC * PER * WIDTH
-    norm_ref[0, 0] = lax.rsqrt(total / count + EPS)[0, 0]
+    out_ref[...] = out_ref[...] * lax.rsqrt(total / count + EPS)[0:1, 0:1]
     drain()
 
 
 def on_device(gen, real):
     dma = pltpu.SemaphoreType.DMA
-    raw, norm = pl.pallas_call(
+    return pl.pallas_call(
         kernel,
-        out_shape=(
-            jax.ShapeDtypeStruct((PER, WIDTH), F32), jax.ShapeDtypeStruct((1, 1), F32),
-        ),
+        out_shape=jax.ShapeDtypeStruct((PER, WIDTH), F32),
         in_specs=[pl.BlockSpec(memory_space=pl.ANY)] * 2,
-        out_specs=(
-            pl.BlockSpec(memory_space=pl.ANY), pl.BlockSpec(memory_space=pltpu.SMEM),
-        ),
+        out_specs=pl.BlockSpec(memory_space=pltpu.VMEM),
         scratch_shapes=[
             pltpu.VMEM((16, PER, WIDTH), BF16),
             pltpu.VMEM((NZ, NC, 2, PER, WIDTH), BF16),
@@ -450,7 +444,6 @@
             pltpu.VMEM((ROWS, 1), F32),
             pltpu.VMEM((NZ, CHUNK), F32),
             pltpu.VMEM((NZ, CHUNK), F32),
-            pltpu.VMEM((PER, WIDTH), F32),
             pltpu.VMEM((16, NZ, CHUNK), F32),
             pltpu.VMEM((16, 4, 128), F32),
             pltpu.VMEM((17, 8, 128), F32),
@@ -464,13 +457,12 @@
             pltpu.VMEM((SLICES, 2, 4, PER, PIECE), BF16),
             pltpu.VMEM((SLICES, 3, PER, PIECE), BF16),
             pltpu.VMEM((SLICES, 3, PER, PIECE), BF16),
-            dma((3,)), dma, dma((SEMS,)), dma((SEMS,)), dma((5,)), dma((5,)),
+            dma((3,)), dma((5,)), dma((SEMS,)), dma((5,)), dma((5,)),
         ],
         compiler_params=pltpu.CompilerParams(
             collective_id=0, has_side_effects=True, vmem_limit_bytes=60 * 1024 * 1024
         ),
     )(gen, real)
-    return raw * norm
 
 
 def solution(mesh):

time: 77.4 us -> 75.5 us (0.975)
  other arithmetic: 2.31 us -> 0 us
  local copies, waits for them, and re-layouts: 0 us -> 1.67 us
  Pallas kernels: 74.9 us -> 73.7 us
    mul x1 -> x0, other arithmetic: 2.31 us -> none  [on_device(): return raw * norm]
    unnamed x0 -> x1, local copies, waits for them, and re-layouts: none -> 1.67 us
    pallas_call x1, Pallas kernels: 74.9 us -> 73.7 us  [on_device(): pl.pallas_call(kernel, out_shape=jax.ShapeDtypeStruct((PER, WIDTH), F32),...]
where the time goes in v3:
time: 75.5 us; the launch traced here: 75.4 us
  Pallas kernels  73.7 us (98%)
  local copies, waits for them, and re-layouts  1.67 us (2%)
    pallas_call x1, Pallas kernels, on_device(): pl.pallas_call(kernel, out_shape=jax.ShapeDtypeStruct((PER, WIDTH), F32),...  73.7 us
    unnamed x1, local copies, waits for them, and re-layouts  1.67 us

profile of v3, /device:TPU:1, one launch (start us, length us, event | category | flops | bytes accessed | tf_op | source)
XLA Modules:
  0.0 75.4 jit_solution(1657581279377045236)
XLA Ops:
  0.0 73.7 %shard_map.28 = f32[32,2048]{1,0:T(8,128)} custom-call(bf16[32,2048]{1,0:T(8,128)(2,1)} %gen_ref.1, bf16[32,2048]{1,0:T(8,128)(2,1)} %real_ref.1), custom_call_target="tpu_custom_call" | custom-call | tf_op jit(solution)/shard_map/pallas_call | solution.py:434
  73.7 1.7 %copy.4 = f32[32,2048]{1,0:T(8,128)} copy(f32[32,2048]{1,0:T(8,128)} %shard_map.28) | data formatting | bytes 524288

commit v4 on v3

--- a/solution.py
+++ b/solution.py
@@ -22,7 +22,7 @@
 F32 = jnp.float32
 BF16 = jnp.bfloat16
 MESH = pl.DeviceIdType.MESH
-SEMS = 104
+SEMS = 41
 
 
 def eye():
@@ -70,7 +70,7 @@
     kinds = ("z", "s", "p", "f", "r")
 
     def drain():
-        sent = (cols.at[pl.ds(0, 7), 0], cols.at[pl.ds(0, 8), 0], rows.at[pl.ds(0, 15)], psend, qsend)
+        sent = (rows.at[pl.ds(0, 14)], rows, rows.at[pl.ds(0, 15)], psend, qsend)
         for k, ref in enumerate(sent):
             pltpu.make_async_copy(ref, ref, ssem.at[k]).wait()
         for k, buf in used:
@@ -79,8 +79,7 @@
 
     def send(key, src, dst, dev):
         k = index.setdefault(key, len(index))
-        assert k == len(index) - 1 and k < SEMS
-        kind = {"q": "p", "i": "f", "d": "f"}.get(key[0][0], key[0][0])
+        kind = {"q": "p", "n": "f"}.get(key[0][0], key[0][0])
         pltpu.make_async_remote_copy(
             src_ref=src, dst_ref=dst, send_sem=ssem.at[kinds.index(kind)], recv_sem=rsem.at[k],
             device_id=dev, device_id_type=MESH,
@@ -91,9 +90,9 @@
 
     own = q * 4 + p
     loads = (
-        pltpu.make_async_copy(gen_ref, rows.at[own], in_sem.at[0]),
-        pltpu.make_async_copy(gen_ref, cols.at[z, c, 0], in_sem.at[1]),
-        pltpu.make_async_copy(real_ref, cols.at[z, c, 1], in_sem.at[2]),
+        pltpu.make_async_copy(gen_ref, rows.at[own], in_sem),
+        pltpu.make_async_copy(gen_ref, cols.at[z, c, 0], in_sem),
+        pltpu.make_async_copy(real_ref, cols.at[z, c, 1], in_sem),
     )
     for copy in loads:
         copy.start()
@@ -105,8 +104,7 @@
     for dev in around:
         pl.semaphore_signal(barrier, inc=1, device_id=dev, device_id_type=MESH)
     pl.semaphore_wait(barrier, len(around))
-    for copy in loads:
-        copy.wait()
+    pltpu.make_async_copy(rows.at[pl.ds(0, 3)], rows.at[pl.ds(0, 3)], in_sem).wait()
 
     top, low = pl.ds(0, HALF), pl.ds(HALF, HALF)
 
@@ -116,58 +114,52 @@
 
     def z_send(d, h, j):
         src, _ = z_piece(d, h - 1, j)
-        send(("z", d, h, j), src, src, at_z(zmod(1 - 2 * d)))
+        send(("z", h, j), src, src, at_z(zmod(1 - 2 * d)))
 
     def z_arrive(h, j):
+        arrived(("z", h, j), cols.at[0, 0, 0])
+        for d in (0, 1):
+            if h < 3 or (h == 3 and j < 2):
+                z_send(d, h + 1, j)
         for d in (0, 1):
             src, kind = z_piece(d, h, j)
-            arrived(("z", d, h, j), src)
-            if h < 3 or (h == 3 and j < 2):
-                z_send(d, h + 1, j)
             if h == 4:
-                send(("s", d, h, j), src, src, sibling)
-            elif j % 2:
+                send(("s", h), src, src, sibling)
+            elif h < 4 and j % 2:
                 whole = cols.at[zmod((2 * d - 1) * h), c, kind]
-                send(("s", d, h, kind), whole, whole, sibling)
+                send(("s", h), whole, whole, sibling)
 
     def sib_arrive(h):
-        for d in (0, 1):
-            zz = zmod((2 * d - 1) * h)
-            if h == 4:
-                for j in (0, 1):
-                    arrived(("s", d, h, j), cols.at[zz, 1 - c, d, low if j else top])
-            elif h or not d:
-                for kind in (0, 1):
-                    arrived(("s", d, h, kind), cols.at[zz, 1 - c, kind])
+        arrived(("s", h), {0: cols.at[0, 0], 4: cols.at[0, 0]}.get(h, cols.at[0]))
 
     def at_row(dq, dp):
         return qmod(dq) * 4 + pmod(dp)
 
     def q_sends(dp):
         block = rows.at[at_row(0, dp)]
-        send(("q", 1, dp), block, block, at_pq(p, qmod(1)))
-        send(("q", -1, dp), block, block, at_pq(p, qmod(-1)))
-
-    def p_arrive(d):
-        arrived(("p", d), rows.at[at_row(0, -d)])
-        half = rows.at[at_row(0, -d), top if d > 0 else low]
-        send(("pf", d), half, half, at_pq(pmod(d), q))
-        q_sends(-d)
+        send(("q", dp), block, block, at_pq(p, qmod(1)))
+        send(("q", dp), block, block, at_pq(p, qmod(-1)))
+
+    def p_arrive():
+        arrived(("p",), rows.at[pl.ds(0, 2)])
+        for d in (1, -1):
+            half = rows.at[at_row(0, -d), top if d > 0 else low]
+            send(("pf",), half, half, at_pq(pmod(d), q))
+        q_sends(-1)
+        q_sends(1)
 
     def p_far():
-        arrived(("pf", 1), rows.at[at_row(0, 2), top])
-        arrived(("pf", -1), rows.at[at_row(0, 2), low])
+        arrived(("pf",), rows.at[0])
         q_sends(2)
 
     def q_arrive(dp):
+        arrived(("q", dp), rows.at[pl.ds(0, 2)])
         for d in (1, -1):
-            arrived(("q", d, dp), rows.at[at_row(-d, dp)])
             half = rows.at[at_row(-d, dp), top if d > 0 else low]
-            send(("qf", d, dp), half, half, at_pq(p, qmod(d)))
+            send(("qf", dp), half, half, at_pq(p, qmod(d)))
 
     def q_far(dp):
-        arrived(("qf", 1, dp), rows.at[at_row(2, dp), top])
-        arrived(("qf", -1, dp), rows.at[at_row(2, dp), low])
+        arrived(("qf", dp), rows.at[0])
 
     def squares_of(value):
         value = value.astype(F32)
@@ -215,10 +207,10 @@
         for d in (0, 1):
             z_send(d, 1, j)
     for d in (1, -1):
-        send(("p", d), rows.at[own], rows.at[own], at_pq(pmod(d), q))
+        send(("p",), rows.at[own], rows.at[own], at_pq(pmod(d), q))
     q_sends(0)
     for kind in (0, 1):
-        send(("s", 0, 0, kind), cols.at[z, c, kind], cols.at[z, c, kind], sibling)
+        send(("s", 0), cols.at[z, c, kind], cols.at[z, c, kind], sibling)
 
     events = []
 
@@ -228,32 +220,31 @@
     for h in range(1, 5):
         for j in range(4 if h < 4 else 2):
             plan(3.0 + 1.4 * ((h - 1) * 4 + j + 1), z_arrive, h, j)
-    plan(4.3, p_arrive, 1)
-    plan(4.3, p_arrive, -1)
-    plan(5.9, q_arrive, 0)
-    plan(8.1, p_far)
-    plan(9.2, q_arrive, -1)
-    plan(10.2, q_arrive, 1)
-    plan(12.5, q_arrive, 2)
-    plan(9.9, q_far, 0)
-    plan(13.0, q_far, -1)
-    plan(14.0, q_far, 1)
-    plan(16.3, q_far, 2)
-    plan(6.0, sib_arrive, 0)
-    plan(6.0, col_squares, 0)
-    plan(8.2, row_squares, 0)
+    plan(4.8, p_arrive)
+    plan(6.5, q_arrive, 0)
+    plan(9.0, p_far)
+    plan(10.0, q_arrive, -1)
+    plan(11.0, q_arrive, 1)
+    plan(11.0, q_far, 0)
+    plan(13.9, q_arrive, 2)
+    plan(15.0, q_far, -1)
+    plan(15.0, q_far, 1)
+    plan(18.6, q_far, 2)
+    plan(6.6, sib_arrive, 0)
+    plan(6.6, col_squares, 0)
+    plan(9.1, row_squares, 0)
     plan(12.6, sib_arrive, 1)
     plan(12.6, col_squares, 1)
-    plan(13.1, col_squares, -1)
-    plan(14.3, row_squares, 1)
-    plan(14.6, row_squares, -1)
-    plan(16.4, row_squares, 2)
-    plan(16.5, tile, 0)
-    plan(17.1, tile, 1, -1)
-    plan(18.5, sib_arrive, 2)
-    plan(18.5, col_squares, 2)
-    plan(18.6, col_squares, -2)
-    plan(19.9, tile, 2, -2)
+    plan(12.6, col_squares, -1)
+    plan(15.6, row_squares, 1)
+    plan(15.6, row_squares, -1)
+    plan(17.1, sib_arrive, 2)
+    plan(17.1, col_squares, 2)
+    plan(17.1, col_squares, -2)
+    plan(18.6, row_squares, 2)
+    plan(18.6, tile, 0)
+    plan(19.9, tile, 1, -1)
+    plan(22.605, tile, 2, -2)
     plan(22.61, sib_arrive, 3)
     plan(22.62, col_squares, 3)
     plan(22.63, col_squares, -3)
@@ -370,43 +361,39 @@
     weigh(across, 0)
     for s in range(SLICES):
         psend[s, 0] = drift(weights[0], s).reshape(4, PER, PIECE).astype(BF16)
-        send(("f", 1, s), psend.at[s, 0, lo], far.at[s, 0], ahead)
-        send(("f", -1, s), psend.at[s, 0, hi], far.at[s, 1], behind)
+        send(("f", s), psend.at[s, 0, lo], far.at[s, 0], ahead)
+        send(("f", s), psend.at[s, 0, hi], far.at[s, 1], behind)
     weigh(after, 1)
     weigh(before, 2)
     for s in range(SLICES):
         part = drift(weights[1:3].reshape(256, COLS), s).reshape(8, PER, PIECE)
         psend[s, 1, 2:4] = part[2:4].astype(BF16)
-        send(("i", 1, s), psend.at[s, 1, hi], near.at[s, 0, hi], ahead)
+        send(("n", s), psend.at[s, 1, hi], near.at[s, 0, hi], ahead)
         psend[s, 2, 0:2] = part[4:6].astype(BF16)
-        send(("i", -1, s), psend.at[s, 2, lo], near.at[s, 1, lo], behind)
+        send(("n", s), psend.at[s, 2, lo], near.at[s, 1, lo], behind)
         kept[s, 0:2] = part[0:2]
         kept[s, 2:4] = part[6:8]
     weigh(q, 0)
     for s in range(SLICES):
         acc[s] = drift(weights[0], s).reshape(4, PER, PIECE)
     for s in range(SLICES):
-        arrived(("f", 1, s), far.at[s, 0])
+        arrived(("f", s), far.at[s])
         psend[s, 1, 0:2] = (kept[s, 0:2] + far[s, 0].astype(F32)).astype(BF16)
-        send(("d", 1, s), psend.at[s, 1, lo], near.at[s, 0, lo], ahead)
-        arrived(("f", -1, s), far.at[s, 1])
+        send(("n", s), psend.at[s, 1, lo], near.at[s, 0, lo], ahead)
         psend[s, 2, 2:4] = (kept[s, 2:4] + far[s, 1].astype(F32)).astype(BF16)
-        send(("d", -1, s), psend.at[s, 2, hi], near.at[s, 1, hi], behind)
-    for s in range(SLICES):
-        arrived(("i", 1, s), near.at[s, 0, hi])
-        arrived(("i", -1, s), near.at[s, 1, lo])
-        arrived(("d", 1, s), near.at[s, 0, lo])
-        arrived(("d", -1, s), near.at[s, 1, hi])
+        send(("n", s), psend.at[s, 2, hi], near.at[s, 1, hi], behind)
+    for s in range(SLICES):
+        arrived(("n", s), near.at[s])
         for d in (2, 1, 3):
             k = pmod(d)
             total = acc[s, k] + near[s, 0, k].astype(F32) + near[s, 1, k].astype(F32)
             qsend[s, d - 1] = total.astype(BF16)
-            send(("r", d, s), qsend.at[s, d - 1], qrecv.at[s, d - 1], at_pq(k, q))
+            send(("r", s), qsend.at[s, d - 1], qrecv.at[s, d - 1], at_pq(k, q))
     square = jnp.zeros((PER, 128), F32)
     for s in range(SLICES):
         total = acc[s, p] + near[s, 0, p].astype(F32) + near[s, 1, p].astype(F32)
+        arrived(("r", s), qrecv.at[s])
         for d in (1, 3, 2):
-            arrived(("r", d, s), qrecv.at[s, d - 1])
             total = total + qrecv[s, d - 1].astype(F32)
         out_ref[:, s * PIECE : (s + 1) * PIECE] = total
         for k in range(PIECE // 128):
@@ -457,7 +444,7 @@
             pltpu.VMEM((SLICES, 2, 4, PER, PIECE), BF16),
             pltpu.VMEM((SLICES, 3, PER, PIECE), BF16),
             pltpu.VMEM((SLICES, 3, PER, PIECE), BF16),
-            dma((3,)), dma((5,)), dma((SEMS,)), dma((5,)), dma((5,)),
+            dma, dma((5,)), dma((SEMS,)), dma((5,)), dma((5,)),
         ],
         compiler_params=pltpu.CompilerParams(
             collective_id=0, has_side_effects=True, vmem_limit_bytes=60 * 1024 * 1024

time: 75.5 us -> 74.8 us (level)
  no operation moved by 1% of the time
where the time goes in v4:
time: 74.8 us; the launch traced here: 74.7 us
  Pallas kernels  73 us (98%)
  local copies, waits for them, and re-layouts  1.67 us (2%)
    pallas_call x1, Pallas kernels, on_device(): pl.pallas_call(kernel, out_shape=jax.ShapeDtypeStruct((PER, WIDTH), F32),...  73 us
    unnamed x1, local copies, waits for them, and re-layouts  1.67 us

profile of v4, /device:TPU:1, one launch (start us, length us, event | category | flops | bytes accessed | tf_op | source)
XLA Modules:
  0.0 74.7 jit_solution(17486532005510040489)
XLA Ops:
  0.0 73.0 %shard_map.28 = f32[32,2048]{1,0:T(8,128)} custom-call(bf16[32,2048]{1,0:T(8,128)(2,1)} %gen_ref.1, bf16[32,2048]{1,0:T(8,128)(2,1)} %real_ref.1), custom_call_target="tpu_custom_call" | custom-call | tf_op jit(solution)/shard_map/pallas_call | solution.py:421
  73.0 1.7 %copy.4 = f32[32,2048]{1,0:T(8,128)} copy(f32[32,2048]{1,0:T(8,128)} %shard_map.28) | data formatting | bytes 524288

commit v5 on v4

--- a/solution.py
+++ b/solution.py
@@ -22,7 +22,7 @@
 F32 = jnp.float32
 BF16 = jnp.bfloat16
 MESH = pl.DeviceIdType.MESH
-SEMS = 41
+SEMS = 44
 
 
 def eye():
@@ -43,7 +43,7 @@
     gen_ref, real_ref, out_ref,
     rows, cols, logits, rsq, rvec, csq, cown,
     cstat, rstat, mstat, n1, n2,
-    weights, psend, acc, kept, far, near, qsend, qrecv,
+    weights, psend, acc, kept, far, near, qsend, qrecv, relay,
     in_sem, ssem, rsem, xs, xr,
 ):
     z, y, c, x = (lax.axis_index(a) for a in AXES)
@@ -79,7 +79,7 @@
 
     def send(key, src, dst, dev):
         k = index.setdefault(key, len(index))
-        kind = {"q": "p", "n": "f"}.get(key[0][0], key[0][0])
+        kind = {"q": "p", "n": "f", "g": "r"}.get(key[0][0], key[0][0])
         pltpu.make_async_remote_copy(
             src_ref=src, dst_ref=dst, send_sem=ssem.at[kinds.index(kind)], recv_sem=rsem.at[k],
             device_id=dev, device_id_type=MESH,
@@ -357,6 +357,7 @@
 
     before, after, across = qmod(-1), qmod(1), qmod(2)
     ahead, behind = at_pq(p, after), at_pq(p, before)
+    p_ahead, p_behind = at_pq(pmod(1), q), at_pq(pmod(-1), q)
     lo, hi = pl.ds(0, 2), pl.ds(2, 2)
     weigh(across, 0)
     for s in range(SLICES):
@@ -384,16 +385,36 @@
         send(("n", s), psend.at[s, 2, hi], near.at[s, 1, hi], behind)
     for s in range(SLICES):
         arrived(("n", s), near.at[s])
-        for d in (2, 1, 3):
-            k = pmod(d)
-            total = acc[s, k] + near[s, 0, k].astype(F32) + near[s, 1, k].astype(F32)
-            qsend[s, d - 1] = total.astype(BF16)
-            send(("r", s), qsend.at[s, d - 1], qrecv.at[s, d - 1], at_pq(k, q))
+        share = [
+            acc[s, pmod(d)] + near[s, 0, pmod(d)].astype(F32) + near[s, 1, pmod(d)].astype(F32)
+            for d in (1, 2, 3)
+        ]
+        if s == SLICES - 1:
+            for d in (2, 1, 3):
+                qsend[s, d - 1] = share[d - 1].astype(BF16)
+                send(("r", s), qsend.at[s, d - 1], qrecv.at[s, d - 1], at_pq(pmod(d), q))
+            continue
+        qsend[s, 1] = share[1].astype(BF16)
+        send(("g", s), qsend.at[s, 1, top], relay.at[s, 0], p_ahead)
+        send(("g", s), qsend.at[s, 1, low], relay.at[s, 1], p_behind)
+        qsend[s, 0, HALF:] = share[0][HALF:].astype(BF16)
+        send(("r", s), qsend.at[s, 0, low], qrecv.at[s, 0, low], p_ahead)
+        qsend[s, 2, :HALF] = share[2][:HALF].astype(BF16)
+        send(("r", s), qsend.at[s, 2, top], qrecv.at[s, 2, top], p_behind)
+        acc[s, pmod(1), :HALF] = share[0][:HALF]
+        acc[s, pmod(3), HALF:] = share[2][HALF:]
+    for s in range(SLICES - 1):
+        arrived(("g", s), relay.at[s])
+        qsend[s, 0, :HALF] = (acc[s, pmod(1), :HALF] + relay[s, 0].astype(F32)).astype(BF16)
+        send(("r", s), qsend.at[s, 0, top], qrecv.at[s, 0, top], p_ahead)
+        qsend[s, 2, HALF:] = (acc[s, pmod(3), HALF:] + relay[s, 1].astype(F32)).astype(BF16)
+        send(("r", s), qsend.at[s, 2, low], qrecv.at[s, 2, low], p_behind)
     square = jnp.zeros((PER, 128), F32)
     for s in range(SLICES):
         total = acc[s, p] + near[s, 0, p].astype(F32) + near[s, 1, p].astype(F32)
-        arrived(("r", s), qrecv.at[s])
-        for d in (1, 3, 2):
+        direct = s == SLICES - 1
+        arrived(("r", s), qrecv.at[s] if direct else qrecv.at[s, pl.ds(0, 2)])
+        for d in (1, 3, 2) if direct else (1, 3):
             total = total + qrecv[s, d - 1].astype(F32)
         out_ref[:, s * PIECE : (s + 1) * PIECE] = total
         for k in range(PIECE // 128):
@@ -444,6 +465,7 @@
             pltpu.VMEM((SLICES, 2, 4, PER, PIECE), BF16),
             pltpu.VMEM((SLICES, 3, PER, PIECE), BF16),
             pltpu.VMEM((SLICES, 3, PER, PIECE), BF16),
+            pltpu.VMEM((SLICES - 1, 2, HALF, PIECE), BF16),
             dma, dma((5,)), dma((SEMS,)), dma((5,)), dma((5,)),
         ],
         compiler_params=pltpu.CompilerParams(

time: 74.8 us -> 75 us (level)
  no operation moved by 1% of the time
where the time goes in v5:
time: 75 us; the launch traced here: 74.9 us
  Pallas kernels  73.2 us (98%)
  local copies, waits for them, and re-layouts  1.67 us (2%)
    pallas_call x1, Pallas kernels, on_device(): pl.pallas_call(kernel, out_shape=jax.ShapeDtypeStruct((PER, WIDTH), F32),...  73.2 us
    unnamed x1, local copies, waits for them, and re-layouts  1.67 us

profile of v5, /device:TPU:1, one launch (start us, length us, event | category | flops | bytes accessed | tf_op | source)
XLA Modules:
  0.0 74.9 jit_solution(8864774218876114997)
XLA Ops:
  0.0 73.2 %shard_map.28 = f32[32,2048]{1,0:T(8,128)} custom-call(bf16[32,2048]{1,0:T(8,128)(2,1)} %gen_ref.1, bf16[32,2048]{1,0:T(8,128)(2,1)} %real_ref.1), custom_call_target="tpu_custom_call" | custom-call | tf_op jit(solution)/shard_map/pallas_call | solution.py:442
  73.2 1.7 %copy.4 = f32[32,2048]{1,0:T(8,128)} copy(f32[32,2048]{1,0:T(8,128)} %shard_map.28) | data formatting | bytes 524288

commit v6 on v4

--- a/solution.py
+++ b/solution.py
@@ -14,7 +14,7 @@
 ROWS = NX * NY * PER
 CHUNK = 2 * NC * PER
 COLS = NZ * CHUNK
-SLICES = 4
+SLICES = 2
 PIECE = WIDTH // SLICES
 INV_SCALE = 1.0 / 0.3
 MASKED = -1e30
@@ -22,7 +22,7 @@
 F32 = jnp.float32
 BF16 = jnp.bfloat16
 MESH = pl.DeviceIdType.MESH
-SEMS = 41
+SEMS = 35
 
 
 def eye():
@@ -77,13 +77,15 @@
             some = buf.at[pl.ds(0, 15)]
             pltpu.make_async_copy(some, some, xs.at[k]).wait()
 
-    def send(key, src, dst, dev):
-        k = index.setdefault(key, len(index))
-        kind = {"q": "p", "n": "f"}.get(key[0][0], key[0][0])
+    def post(k, kind, src, dst, dev):
         pltpu.make_async_remote_copy(
             src_ref=src, dst_ref=dst, send_sem=ssem.at[kinds.index(kind)], recv_sem=rsem.at[k],
             device_id=dev, device_id_type=MESH,
         ).start()
+
+    def send(key, src, dst, dev):
+        k = index.setdefault(key, len(index))
+        post(k, {"q": "p"}.get(key[0][0], key[0][0]), src, dst, dev)
 
     def arrived(key, ref):
         pltpu.make_async_copy(ref, ref, rsem.at[index[key]]).wait()
@@ -181,16 +183,25 @@
     zc = z * NC + c
 
     def tile(*ds):
-        rhs = [cols[zmod(d)].reshape(CHUNK, WIDTH) for d in ds]
-        rhs = jnp.concatenate(rhs, axis=0) if len(rhs) > 1 else rhs[0]
-        inner = lax.dot_general(
-            rows[...].reshape(ROWS, WIDTH), rhs, (((1,), (1,)), ((), ())),
-            preferred_element_type=F32,
-        )
-        for k, d in enumerate(ds):
-            gap = rsq[...] + csq[pl.ds(zmod(d), 1), :] - 2.0 * inner[:, k * CHUNK : (k + 1) * CHUNK]
-            gap = jnp.maximum(gap, 1.0)
-            logits[:, lanes_of(d)] = gap * lax.rsqrt(gap) * -INV_SCALE
+        def rhs():
+            parts = [cols[zmod(d)].reshape(CHUNK, WIDTH) for d in ds]
+            return jnp.concatenate(parts, axis=0) if len(parts) > 1 else parts[0]
+
+        block_rows = ROWS // 2
+
+        def some_rows(b, carry):
+            part = pl.ds(pl.multiple_of(b * block_rows, block_rows), block_rows)
+            lhs = rows[pl.ds(b * 8, 8)].reshape(block_rows, WIDTH)
+            inner = lax.dot_general(
+                lhs, rhs(), (((1,), (1,)), ((), ())), preferred_element_type=F32
+            )
+            for k, d in enumerate(ds):
+                gap = rsq[part, :] + csq[pl.ds(zmod(d), 1), :]
+                gap = jnp.maximum(gap - 2.0 * inner[:, k * CHUNK : (k + 1) * CHUNK], 1.0)
+                logits[part, lanes_of(d)] = gap * lax.rsqrt(gap) * -INV_SCALE
+            return carry
+
+        lax.fori_loop(0, 2, some_rows, 0)
         if ds == (0,):
             mine = pl.ds(pl.multiple_of(own * PER, PER), PER)
             block = logits[mine, lanes_of(0)]
@@ -351,54 +362,85 @@
             half = logits[part, j * CHUNK : (j + 1) * CHUNK] * cown[j : j + 1, :]
             weights[at, :, j * CHUNK : (j + 1) * CHUNK] = (half * scale).astype(BF16)
 
+    def lanes(s):
+        return pl.ds(pl.multiple_of(s * PIECE, PIECE), PIECE)
+
     def drift(w, s):
-        samples = cols[:, :, :, :, s * PIECE : (s + 1) * PIECE].reshape(COLS, PIECE)
+        samples = cols[:, :, :, :, lanes(s)].reshape(COLS, PIECE)
         return jnp.dot(w, samples, preferred_element_type=F32)
+
+    def each(body):
+        def one(s, carry):
+            body(s)
+            return carry
+        lax.fori_loop(0, SLICES, one, 0)
+
+    far_sem = len(index)
+    near_sem, last_sem = far_sem + SLICES, far_sem + 2 * SLICES
+    assert last_sem + SLICES == SEMS
 
     before, after, across = qmod(-1), qmod(1), qmod(2)
     ahead, behind = at_pq(p, after), at_pq(p, before)
     lo, hi = pl.ds(0, 2), pl.ds(2, 2)
     weigh(across, 0)
-    for s in range(SLICES):
+
+    def far_part(s):
         psend[s, 0] = drift(weights[0], s).reshape(4, PER, PIECE).astype(BF16)
-        send(("f", s), psend.at[s, 0, lo], far.at[s, 0], ahead)
-        send(("f", s), psend.at[s, 0, hi], far.at[s, 1], behind)
+        post(far_sem + s, "f", psend.at[s, 0, lo], far.at[s, 0], ahead)
+        post(far_sem + s, "f", psend.at[s, 0, hi], far.at[s, 1], behind)
+
+    each(far_part)
     weigh(after, 1)
     weigh(before, 2)
-    for s in range(SLICES):
+
+    def near_part(s):
         part = drift(weights[1:3].reshape(256, COLS), s).reshape(8, PER, PIECE)
         psend[s, 1, 2:4] = part[2:4].astype(BF16)
-        send(("n", s), psend.at[s, 1, hi], near.at[s, 0, hi], ahead)
+        post(near_sem + s, "f", psend.at[s, 1, hi], near.at[s, 0, hi], ahead)
         psend[s, 2, 0:2] = part[4:6].astype(BF16)
-        send(("n", s), psend.at[s, 2, lo], near.at[s, 1, lo], behind)
+        post(near_sem + s, "f", psend.at[s, 2, lo], near.at[s, 1, lo], behind)
         kept[s, 0:2] = part[0:2]
         kept[s, 2:4] = part[6:8]
+
+    each(near_part)
     weigh(q, 0)
-    for s in range(SLICES):
+
+    def own_part(s):
         acc[s] = drift(weights[0], s).reshape(4, PER, PIECE)
-    for s in range(SLICES):
-        arrived(("f", s), far.at[s])
+
+    each(own_part)
+
+    def relay(s):
+        pltpu.make_async_copy(far.at[s], far.at[s], rsem.at[far_sem + s]).wait()
         psend[s, 1, 0:2] = (kept[s, 0:2] + far[s, 0].astype(F32)).astype(BF16)
-        send(("n", s), psend.at[s, 1, lo], near.at[s, 0, lo], ahead)
+        post(near_sem + s, "f", psend.at[s, 1, lo], near.at[s, 0, lo], ahead)
         psend[s, 2, 2:4] = (kept[s, 2:4] + far[s, 1].astype(F32)).astype(BF16)
-        send(("n", s), psend.at[s, 2, hi], near.at[s, 1, hi], behind)
-    for s in range(SLICES):
-        arrived(("n", s), near.at[s])
+        post(near_sem + s, "f", psend.at[s, 2, hi], near.at[s, 1, hi], behind)
+
+    each(relay)
+
+    def last_part(s):
+        pltpu.make_async_copy(near.at[s], near.at[s], rsem.at[near_sem + s]).wait()
         for d in (2, 1, 3):
             k = pmod(d)
             total = acc[s, k] + near[s, 0, k].astype(F32) + near[s, 1, k].astype(F32)
             qsend[s, d - 1] = total.astype(BF16)
-            send(("r", s), qsend.at[s, d - 1], qrecv.at[s, d - 1], at_pq(k, q))
-    square = jnp.zeros((PER, 128), F32)
-    for s in range(SLICES):
+            post(last_sem + s, "r", qsend.at[s, d - 1], qrecv.at[s, d - 1], at_pq(k, q))
+
+    each(last_part)
+
+    def finish(s, square):
         total = acc[s, p] + near[s, 0, p].astype(F32) + near[s, 1, p].astype(F32)
-        arrived(("r", s), qrecv.at[s])
+        pltpu.make_async_copy(qrecv.at[s], qrecv.at[s], rsem.at[last_sem + s]).wait()
         for d in (1, 3, 2):
             total = total + qrecv[s, d - 1].astype(F32)
-        out_ref[:, s * PIECE : (s + 1) * PIECE] = total
+        out_ref[:, lanes(s)] = total
         for k in range(PIECE // 128):
             lane = total[:, k * 128 : (k + 1) * 128]
             square = square + lane * lane
+        return square
+
+    square = lax.fori_loop(0, SLICES, finish, jnp.zeros((PER, 128), F32))
     n1[zc] = jnp.broadcast_to(jnp.sum(square, keepdims=True), (1, 128))
     first_known = exchange(n1, zc, z_peers)
     first_known()

time: 74.8 us -> 73.6 us (0.984)
  Pallas kernels: 73 us -> 71.8 us
    pallas_call x1, Pallas kernels: 73 us -> 71.8 us  [on_device(): pl.pallas_call(kernel, out_shape=jax.ShapeDtypeStruct((PER, WIDTH), F32),...]
where the time goes in v6:
time: 73.6 us; the launch traced here: 73.5 us
  Pallas kernels  71.8 us (98%)
  local copies, waits for them, and re-layouts  1.67 us (2%)
    pallas_call x1, Pallas kernels, on_device(): pl.pallas_call(kernel, out_shape=jax.ShapeDtypeStruct((PER, WIDTH), F32),...  71.8 us
    unnamed x1, local copies, waits for them, and re-layouts  1.67 us

profile of v6, /device:TPU:1, one launch (start us, length us, event | category | flops | bytes accessed | tf_op | source)
XLA Modules:
  0.0 73.5 jit_solution(15480257356157722470)
XLA Ops:
  0.0 71.8 %shard_map.28 = f32[32,2048]{1,0:T(8,128)} custom-call(bf16[32,2048]{1,0:T(8,128)(2,1)} %gen_ref.1, bf16[32,2048]{1,0:T(8,128)(2,1)} %real_ref.1), custom_call_target="tpu_custom_call" | custom-call | tf_op jit(solution)/shard_map/pallas_call | solution.py:463
  71.8 1.7 %copy.4 = f32[32,2048]{1,0:T(8,128)} copy(f32[32,2048]{1,0:T(8,128)} %shard_map.28) | data formatting | bytes 524288

commit v7 on v6

--- a/solution.py
+++ b/solution.py
@@ -187,11 +187,12 @@
             parts = [cols[zmod(d)].reshape(CHUNK, WIDTH) for d in ds]
             return jnp.concatenate(parts, axis=0) if len(parts) > 1 else parts[0]
 
-        block_rows = ROWS // 2
+        n = 1 if ds == (4,) else 2
+        block_rows = ROWS // n
 
         def some_rows(b, carry):
             part = pl.ds(pl.multiple_of(b * block_rows, block_rows), block_rows)
-            lhs = rows[pl.ds(b * 8, 8)].reshape(block_rows, WIDTH)
+            lhs = rows[pl.ds(b * (16 // n), 16 // n)].reshape(block_rows, WIDTH)
             inner = lax.dot_general(
                 lhs, rhs(), (((1,), (1,)), ((), ())), preferred_element_type=F32
             )
@@ -201,7 +202,7 @@
                 logits[part, lanes_of(d)] = gap * lax.rsqrt(gap) * -INV_SCALE
             return carry
 
-        lax.fori_loop(0, 2, some_rows, 0)
+        lax.fori_loop(0, n, some_rows, 0)
         if ds == (0,):
             mine = pl.ds(pl.multiple_of(own * PER, PER), PER)
             block = logits[mine, lanes_of(0)]
@@ -266,7 +267,7 @@
     col_squares(4)
     tile(4)
 
-    z_order = [(d, k) for d in (4, 3, -3, 2, -2, 1, -1, 0) for k in (1, 0) if d or k]
+    z_order = [(d, k) for d in (4, 3, -3, 2, -2, 1, -1, 0) for k in (0, 1) if d or k]
     pq_order = sorted(
         ((i, j) for i in range(4) for j in range(4) if i or j),
         key=lambda d: -min(d[0], 4 - d[0]) - min(d[1], 4 - d[1]),
@@ -408,7 +409,6 @@
     def own_part(s):
         acc[s] = drift(weights[0], s).reshape(4, PER, PIECE)
 
-    each(own_part)
 
     def relay(s):
         pltpu.make_async_copy(far.at[s], far.at[s], rsem.at[far_sem + s]).wait()
@@ -417,7 +417,11 @@
         psend[s, 2, 2:4] = (kept[s, 2:4] + far[s, 1].astype(F32)).astype(BF16)
         post(near_sem + s, "f", psend.at[s, 2, hi], near.at[s, 1, hi], behind)
 
-    each(relay)
+    def relay_then_own(s):
+        relay(s)
+        own_part(s)
+
+    each(relay_then_own)
 
     def last_part(s):
         pltpu.make_async_copy(near.at[s], near.at[s], rsem.at[near_sem + s]).wait()

time: 73.6 us -> 72.7 us (0.988)
  Pallas kernels: 71.8 us -> 70.9 us
    pallas_call x1, Pallas kernels: 71.8 us -> 70.9 us  [on_device(): pl.pallas_call(kernel, out_shape=jax.ShapeDtypeStruct((PER, WIDTH), F32),...]
where the time goes in v7:
time: 72.7 us; the launch traced here: 72.6 us
  Pallas kernels  70.9 us (98%)
  local copies, waits for them, and re-layouts  1.67 us (2%)
    pallas_call x1, Pallas kernels, on_device(): pl.pallas_call(kernel, out_shape=jax.ShapeDtypeStruct((PER, WIDTH), F32),...  70.9 us
    unnamed x1, local copies, waits for them, and re-layouts  1.67 us

profile of v7, /device:TPU:1, one launch (start us, length us, event | category | flops | bytes accessed | tf_op | source)
XLA Modules:
  0.0 72.6 jit_solution(1160433669098373528)
XLA Ops:
  0.0 70.9 %shard_map.28 = f32[32,2048]{1,0:T(8,128)} custom-call(bf16[32,2048]{1,0:T(8,128)(2,1)} %gen_ref.1, bf16[32,2048]{1,0:T(8,128)(2,1)} %real_ref.1), custom_call_target="tpu_custom_call" | custom-call | tf_op jit(solution)/shard_map/pallas_call | solution.py:467
  70.9 1.7 %copy.4 = f32[32,2048]{1,0:T(8,128)} copy(f32[32,2048]{1,0:T(8,128)} %shard_map.28) | data formatting | bytes 524288

commit v8 on v7

--- a/solution.py
+++ b/solution.py
@@ -425,7 +425,7 @@
 
     def last_part(s):
         pltpu.make_async_copy(near.at[s], near.at[s], rsem.at[near_sem + s]).wait()
-        for d in (2, 1, 3):
+        for d in (1, 3, 2):
             k = pmod(d)
             total = acc[s, k] + near[s, 0, k].astype(F32) + near[s, 1, k].astype(F32)
             qsend[s, d - 1] = total.astype(BF16)

time: 72.7 us -> 72.5 us (level)
  no operation moved by 1% of the time
where the time goes in v8:
time: 72.5 us; the launch traced here: 72.4 us
  Pallas kernels  70.8 us (98%)
  local copies, waits for them, and re-layouts  1.67 us (2%)
    pallas_call x1, Pallas kernels, on_device(): pl.pallas_call(kernel, out_shape=jax.ShapeDtypeStruct((PER, WIDTH), F32),...  70.8 us
    unnamed x1, local copies, waits for them, and re-layouts  1.67 us

profile of v8, /device:TPU:1, one launch (start us, length us, event | category | flops | bytes accessed | tf_op | source)
XLA Modules:
  0.0 72.4 jit_solution(8090870244620979372)
XLA Ops:
  0.0 70.8 %shard_map.28 = f32[32,2048]{1,0:T(8,128)} custom-call(bf16[32,2048]{1,0:T(8,128)(2,1)} %gen_ref.1, bf16[32,2048]{1,0:T(8,128)(2,1)} %real_ref.1), custom_call_target="tpu_custom_call" | custom-call | tf_op jit(solution)/shard_map/pallas_call | solution.py:467
  70.8 1.7 %copy.4 = f32[32,2048]{1,0:T(8,128)} copy(f32[32,2048]{1,0:T(8,128)} %shard_map.28) | data formatting | bytes 524288
